TPU v7x, 256 devices: a whole 4x4x8 slice. The times are simulated.
256 devices in a mesh: rows: 8 (over y, core), cols: 16 (over z_hi, x), hub: 2 (over z_lo).
Axes of the slice: x: 4, y: 4, z: 8 (z_hi: 4, z_lo: 2; z = z_hi * 2 + z_lo), core: 2. Of those that a mesh axis runs over, the one named last changes fastest.
Arguments:
- light_bits: int32 [384, 12288], P('rows', 'cols'), may hold values from -2147483648 to 2147483647, as said below
- hub_bits: int32 [8, 12288], P('hub', 'cols'), may hold values from -2147483648 to 2147483647, as said below
- hub_ids: int32 [256], replicated, may hold values from 0 to 12287, as said below
Outputs:
- clustering: float32 [12288], P(('rows', 'cols'))
Inputs may be any that keep to these rules, and one draw needn't show every extreme that they name: Every word holds 32 bits; the matrix of light_bits is symmetric with a zero diagonal. `hub_bits`: every word holds 32 bits. `hub_ids`: 256 distinct vertex numbers.
All inputs are finite; a program needn't handle non-finite values.
Results may differ from a plain program's by a relative error of at most 0.0003.
Values sent between devices are 32-bit elements; how exact they have to be, the bound alone decides.
A program may use at most 128 MiB of HBM per device.

v0:
```python
import jax
import jax.numpy as jnp
from jax import lax
from jax.sharding import Mesh
from jax.sharding import PartitionSpec as P

ROWS = ("rows_0", "rows_1")
COLS = ("cols_0", "cols_1")
ROWS_COLS_HUB = ("rows_0", "rows_1", "cols_0", "cols_1", "hub")
COLS_HUB = ("cols_0", "cols_1", "hub")
ROWS_COLS = ("rows_0", "rows_1", "cols_0", "cols_1")


def in_order(pieces, dim):
    pieces = jnp.moveaxis(pieces, 0, dim)
    shape = pieces.shape
    return pieces.reshape(*shape[:dim], shape[dim] * shape[dim + 1], *shape[dim + 2 :])


def from_everyone(value, axis):
    copies = jnp.broadcast_to(value, (lax.axis_size(axis), *value.shape))
    return lax.all_to_all(copies, axis, split_axis=0, concat_axis=0, tiled=True)


def gathered_copies(value, axis, dim):
    return in_order(from_everyone(value, axis), dim)


def by_axis(value, axes):
    for axis in axes:
        value = lax.psum(value, axis)
    return value


def of_everyone(value, axis):
    everything = from_everyone(value, axis)
    return jnp.sum(everything, axis=0)


def together(arrays, axis):
    vector, at, done = (jnp.concatenate([a.reshape(-1) for a in arrays]), 0, [])
    running = of_everyone(vector, axis)
    for a in arrays:
        done.append(running[at : at + a.size].reshape(a.shape))
        at += a.size
    return tuple(done)


def unpack(packed):
    shifts = jnp.arange(32, dtype=jnp.int32)
    bit_grid = jnp.bitwise_and(jnp.right_shift(packed[:, None, :], shifts[None, :, None]), 1)
    return bit_grid.reshape(packed.shape[0] * 32, packed.shape[1]).astype(jnp.bfloat16)


def light_flags(anchor, amount, hub_ids):
    vertex_ids = anchor + lax.iota(jnp.int32, amount)
    is_hub = jnp.any(vertex_ids[:, None] == hub_ids[None, :], axis=1)
    return jnp.where(is_hub, 0.0, 1.0).astype(jnp.bfloat16)


def body(light_bits, hub_bits, hub_ids):
    row_idx = lax.axis_index(ROWS)
    col_idx = lax.axis_index(COLS)
    group_idx = lax.axis_index("hub")
    groups = lax.axis_size("hub")
    col_devices = lax.axis_size(COLS)
    block_words = light_bits.shape[0]
    block_rows = 32 * block_words
    block_cols = light_bits.shape[1]
    row_base = row_idx * block_rows
    col_base = col_idx * block_cols
    row_keep = light_flags(row_base, block_rows, hub_ids)
    col_keep = light_flags(col_base, block_cols, hub_ids)
    adjacent = unpack(light_bits) * row_keep[:, None] * col_keep[None, :]
    part_words = block_words // groups
    part_rows = 32 * part_words
    row_start = group_idx * part_rows
    row_words = lax.dynamic_slice_in_dim(light_bits, group_idx * part_words, part_words, 0)
    col_start = 0
    row_keep_part = lax.dynamic_slice_in_dim(row_keep, row_start, part_rows, 0)
    row_packed = lax.all_gather(row_words, COLS, axis=1, tiled=True)
    section = gathered_copies(light_bits, ROWS, 0)
    vertex_start = 32 * jnp.int32(0)
    section_rows = 32 * section.shape[0]
    keep_mid = light_flags(vertex_start, section_rows, hub_ids)
    column_bits = unpack(section) * keep_mid[:, None]
    row_slice = unpack(row_packed)
    two_paths = jnp.dot(row_slice, column_bits, preferred_element_type=jnp.float32)
    two_paths = two_paths * row_keep_part.astype(jnp.float32)[:, None]
    own_part = lax.dynamic_slice(adjacent, (row_start, col_start), (part_rows, block_cols)).astype(
        jnp.float32
    )
    light_tri = 0.5 * jnp.sum(own_part * two_paths, axis=1)
    light_deg = jnp.sum(own_part, axis=1)
    tri_vec = lax.dynamic_update_slice_in_dim(
        jnp.zeros((block_rows,), jnp.float32), light_tri, row_start, 0
    )
    deg_vec = lax.dynamic_update_slice_in_dim(
        jnp.zeros((block_rows,), jnp.float32), light_deg, row_start, 0
    )
    group_hubs = 32 * hub_bits.shape[0]
    hub_cols = unpack(hub_bits) * col_keep[None, :]
    hub_whole = gathered_copies(hub_bits, COLS, 1)
    hub_here = (
        unpack(lax.dynamic_slice_in_dim(hub_whole, row_base, block_rows, 1)) * row_keep[None, :]
    )
    reach_hub = lax.dot_general(
        hub_cols, adjacent, (((1,), (1,)), ((), ())), preferred_element_type=jnp.float32
    )
    intersect = hub_here.astype(jnp.float32) * reach_hub
    first_col = (col_idx == 0).astype(jnp.float32)
    first_row = (row_idx == 0).astype(jnp.float32)
    tri_vec = tri_vec + jnp.sum(intersect, axis=0)
    deg_vec = deg_vec + first_col * jnp.sum(hub_here.astype(jnp.float32), axis=0)
    hub_tri = 0.5 * jnp.sum(intersect, axis=1)
    hub_deg = first_row * jnp.sum(hub_cols.astype(jnp.float32), axis=1)
    all_hubs = hub_ids.shape[0]
    hub_tri_full = lax.dynamic_update_slice_in_dim(
        jnp.zeros((all_hubs,), jnp.float32), hub_tri, group_idx * group_hubs, 0
    )
    hub_deg_full = lax.dynamic_update_slice_in_dim(
        jnp.zeros((all_hubs,), jnp.float32), hub_deg, group_idx * group_hubs, 0
    )
    hub_tri_full, hub_deg_full = (
        by_axis(hub_tri_full, ROWS_COLS_HUB),
        by_axis(hub_deg_full, ROWS_COLS_HUB),
    )
    per_device = block_rows // col_devices
    tri_whole, deg_whole = together((tri_vec, deg_vec), COLS_HUB)
    tri_mine = lax.dynamic_slice_in_dim(tri_whole, col_idx * per_device, per_device, 0)
    deg_mine = lax.dynamic_slice_in_dim(deg_whole, col_idx * per_device, per_device, 0)
    vertex_ids = row_base + col_idx * per_device + lax.iota(jnp.int32, per_device)
    owners = (vertex_ids[:, None] == hub_ids[None, :]).astype(jnp.float32)
    tri_mine = tri_mine + jnp.sum(owners * hub_tri_full[None, :], axis=1)
    deg_mine = deg_mine + jnp.sum(owners * hub_deg_full[None, :], axis=1)
    return tri_mine / (1.0 + deg_mine)


def solution(mesh):
    finer = Mesh(
        mesh.devices.reshape(4, 2, 4, 4, mesh.shape["hub"]),
        ("rows_0", "rows_1", "cols_0", "cols_1", "hub"),
    )
    placed = (P(ROWS, COLS), P("hub", COLS), P())
    return jax.shard_map(body, mesh=finer, in_specs=placed, out_specs=P(ROWS_COLS), check_vma=False)
```

profile of v0, /device:TPU:8, one launch (start us, length us, event | category | flops | bytes accessed | tf_op | source)
XLA Modules:
  0.0 156.2 jit_solution(6811426682850002151)
XLA Ops:
  6.5 0.0 all-gather.2.cloned.1.call-start
  6.5 1.5 constant_dynamic-slice_fusion
  8.1 0.0 all-gather.2.cloned.1.call-update
  8.1 1.4 broadcast_in_dim.28
  9.5 11.0 %all-to-all-start = ((s32[16,4,768]{2,1,0:T(4,128)}), s32[16,4,768]{2,1,0:T(4,128)S(1)}, u32[]{:S(2)}, u32[]{:S(2)}) async-start(s32[16,4,768]{2,1,0:T(4,128)} %broadcast_in_dim.28), calls=%async_computation | async-start | bytes 393216 | tf_op jit(solution)/shard_map/all_to_all | solution.py:22
  20.5 2.6 %fusion.1 = pred[12288]{0:T(1024)(128)(4,1)S(1)} fusion(s32[256]{0:T(256)} %param.5), kind=kLoop, calls=%fused_computation.4 | loop fusion | flops 6279168 | bytes 13312 | tf_op jit(solution)/shard_map/reduce_or | solution.py:57
  23.1 1.0 compare_reduce_fusion.1
  24.1 0.0 copy-start.4
  24.1 1.2 compare_reduce_fusion
  25.3 0.1 shift_right_arithmetic.136
  25.4 0.7 fusion.15
  26.1 0.1 dynamic-slice.2
  26.2 1.3 shift_right_arithmetic.131
  27.5 1.6 %constant_dynamic-slice_fusion.1 = s32[768,768]{1,0:T(8,128)} fusion(s32[1536,768]{1,0:T(8,128)S(1)} %bitcast.23, s32[]{:T(128)S(6)} %select_n.54), kind=kLoop, calls=%fused_computation.42 | loop fusion | bytes 4718596 | tf_op jit(solution)/shard_map/dynamic_slice | solution.py:90
  29.0 2.0 %copy.15 = s32[768,768]{0,1:T(8,128)S(1)} copy(s32[768,768]{1,0:T(8,128)} %constant_dynamic-slice_fusion.1) | data formatting | bytes 4718592
  31.1 0.0 copy-start.2
  31.1 0.0 copy-start
  31.1 0.0 copy-done.9
  31.1 0.0 copy-done.6
  31.1 1.1 convert_reduce_fusion
  32.2 0.0 copy-done.2
  32.2 0.7 fusion.11
  32.9 0.1 convert_element_type.113
  33.0 0.6 shift_right_arithmetic.125
  33.6 0.7 convert_element_type.120
  34.3 0.0 copy-done.4
  34.3 0.0 copy-done
  34.3 2.3 %fusion.4 = bf16[48,32,768]{2,1,0:T(8,128)(2,1)} fusion(s32[48,768]{1,0:T(8,128)S(1)} %copy-done, bf16[768]{0:T(1024)(128)(2,1)S(1)} %select_convert_fusion.2, bf16[48,32]{1,0:T(8,128)(2,1)S(1)} %convert_element_type.113), kind=kLoop, calls=%fused_computation.11 | loop fusion | flops 10616832 | bytes 2511360 | tf_op jit(solution)/shard_map/mul | solution.py:74
  36.6 0.0 all-to-all-done
  36.6 1.1 broadcast_in_dim.32
  37.8 4.9 %all-to-all-start.1 = ((s32[8,48,768]{2,1,0:T(8,128)}), s32[8,48,768]{2,1,0:T(8,128)S(1)}, u32[]{:S(2)}, u32[]{:S(2)}) async-start(s32[8,48,768]{2,1,0:T(8,128)} %broadcast_in_dim.32), calls=%async_computation.1 | async-start | bytes 2359296 | tf_op jit(solution)/shard_map/all_to_all | solution.py:22
  42.7 0.7 constant_dynamic-slice_fusion.2
  43.4 0.8 fusion.10
  44.3 0.1 convert_reduce_fusion.1
  44.4 0.6 broadcast_multiply_fusion
  45.0 1.5 add_dynamic-update-slice_fusion
  46.5 3.4 %fusion.14 = (f32[128]{0:T(128)S(1)}, f32[1536]{0:T(1024)}) fusion(bf16[128,768]{1,0:T(8,128)(2,1)} %bitcast.26, bf16[1536,768]{1,0:T(8,128)(2,1)} %bitcast.24, bf16[128,1536]{1,0:T(8,128)(2,1)S(1)} %fusion.10), kind=kOutput, calls=%fused_computation.47 | convolution fusion | flops 302774656 | bytes 2955776 | tf_op jit(solution)/shard_map/dot_general | solution.py:107
  49.9 8.7 %all-to-all-done.1 = s32[8,48,768]{2,1,0:T(8,128)S(1)} async-done(((s32[8,48,768]{2,1,0:T(8,128)}), s32[8,48,768]{2,1,0:T(8,128)S(1)}, u32[]{:S(2)}, u32[]{:S(2)}) %all-to-all-start.1) | async-done | bytes 1179680 | tf_op jit(solution)/shard_map/all_to_all | solution.py:22
  58.6 9.2 %fusion = bf16[384,32,768]{2,1,0:T(8,128)(2,1)} fusion(s32[384,768]{1,0:T(8,128)S(1)} %bitcast.25, bf16[384,32]{1,0:T(8,128)(2,1)} %convert_element_type.120), kind=kLoop, calls=%fused_computation.2 | loop fusion | flops 66060288 | bytes 20078592 | tf_op jit(solution)/shard_map/mul | solution.py:86
  67.8 0.0 copy-start.11
  67.8 0.0 all-gather.2.cloned.1.call-done
  67.8 8.0 %and_convert_fusion.1 = bf16[24,32,12288]{2,1,0:T(8,128)(2,1)} fusion(s32[24,12288]{1,0:T(8,128)} %all-gather.2.cloned.1.call-done), kind=kLoop, calls=%fused_computation.1 | loop fusion | flops 28311552 | bytes 20054016 | tf_op jit(solution)/shard_map/convert_element_type | solution.py:52
  75.8 0.0 copy-done.7
  75.8 0.0 copy-start.8
  75.8 20.7 %fusion.2 = f32[768]{0:T(1024)S(1)} fusion(bf16[768,12288]{1,0:T(8,128)(2,1)} %bitcast.22, bf16[12288,768]{1,0:T(8,128)(2,1)} %bitcast.21, f32[768]{0:T(1024)S(1)} %copy-done.11, bf16[768]{0:T(1024)(128)(2,1)S(1)} %copy-done.5, bf16[768]{0:T(1024)(128)(2,1)S(1)} %copy-done.10, s32[768,768]{0,1:T(8,128)S(1)} %copy.15, s32[768]{0:T(1024)S(1)} %copy-done.7), kind=kOutput, calls=%fused_computation.9 | convolution fusion | flops 14502591488 | bytes 40120320 | tf_op jit(solution)/shard_map/dot_general | solution.py:88
  96.5 0.0 copy-done.3
  96.5 0.2 add_dynamic-update-slice_fusion.1
  96.7 0.7 pad_maximum_fusion
  97.4 0.9 broadcast_in_dim.35
  98.3 9.9 %all-to-all-start.2 = ((f32[32,1,3072]{2,1,0:T(1,128)}), f32[32,1,3072]{2,1,0:T(1,128)S(1)}, u32[]{:S(2)}, u32[]{:S(2)}) async-start(f32[32,1,3072]{2,1,0:T(1,128)} %broadcast_in_dim.35), calls=%async_computation.2 | async-start | bytes 786432 | tf_op jit(solution)/shard_map/all_to_all | solution.py:22
  108.2 0.1 convert_reduce_fusion.2
  108.4 0.1 mul.216
  108.5 0.2 dynamic_update_slice.15
  108.7 0.1 multiply_dynamic-update-slice_fusion
  108.8 9.2 %all-reduce.2 = (f32[256]{0:T(256)S(1)}, f32[256]{0:T(256)S(1)}) all-reduce(f32[256]{0:T(256)S(1)} %multiply_dynamic-update-slice_fusion, f32[256]{0:T(256)S(1)} %dynamic_update_slice.15), channel_id=1, replica_groups=mesh['rows_0'=4,'rows_1'=2,'cols_0'=4,'cols_1'=4,'hub'=2] {'rows_0'}, use_global_device_ids=true, to_apply=%region_9.10 | all-reduce | flops 512 | bytes 4096 | tf_op jit(solution)/shard_map/psum | solution.py:31
  117.9 2.5 %all-reduce.4 = (f32[256]{0:T(256)S(1)}, f32[256]{0:T(256)S(1)}) all-reduce(f32[256]{0:T(256)S(1)} %get-tuple-element.13, f32[256]{0:T(256)S(1)} %get-tuple-element.14), channel_id=1, replica_groups=mesh['rows_0'=4,'rows_1'=2,'cols_0'=4,'cols_1'=4,'hub'=2] {'rows_1'}, use_global_device_ids=true, to_apply=%region_10.11 | all-reduce | flops 512 | bytes 4096 | tf_op jit(solution)/shard_map/psum | solution.py:31
  120.4 12.6 %all-reduce.1 = (f32[256]{0:T(256)S(1)}, f32[256]{0:T(256)S(1)}) all-reduce(f32[256]{0:T(256)S(1)} %get-tuple-element.17, f32[256]{0:T(256)S(1)} %get-tuple-element.18), channel_id=1, replica_groups=mesh['rows_0'=4,'rows_1'=2,'cols_0'=4,'cols_1'=4,'hub'=2] {'cols_0'}, use_global_device_ids=true, to_apply=%region_11.12 | all-reduce | flops 512 | bytes 4096 | tf_op jit(solution)/shard_map/psum | solution.py:31
  133.0 10.4 %all-reduce = (f32[256]{0:T(256)S(1)}, f32[256]{0:T(256)S(1)}) all-reduce(f32[256]{0:T(256)S(1)} %get-tuple-element.11, f32[256]{0:T(256)S(1)} %get-tuple-element.12), channel_id=1, replica_groups=mesh['rows_0'=4,'rows_1'=2,'cols_0'=4,'cols_1'=4,'hub'=2] {'cols_1'}, use_global_device_ids=true, to_apply=%region_12.13 | all-reduce | flops 512 | bytes 4096 | tf_op jit(solution)/shard_map/psum | solution.py:31
  143.4 4.9 %all-reduce.3 = (f32[256]{0:T(256)S(1)}, f32[256]{0:T(256)S(1)}) all-reduce(f32[256]{0:T(256)S(1)} %get-tuple-element.9, f32[256]{0:T(256)S(1)} %get-tuple-element.10), channel_id=1, replica_groups=mesh['rows_0'=4,'rows_1'=2,'cols_0'=4,'cols_1'=4,'hub'=2] {'hub'}, use_global_device_ids=true, to_apply=%region_13.14 | all-reduce | flops 512 | bytes 4096 | tf_op jit(solution)/shard_map/psum | solution.py:31
  148.3 0.0 copy-done.8
  148.3 0.2 fusion.12
  148.5 0.0 all-to-all-done.2
  148.5 0.2 reduce_sum.88
  148.7 0.6 add_divide_fusion
  (23 shorter events, 0.1 us)
Async XLA Ops:
  6.5 61.2 %all-gather.2.cloned.1.call-start = ((), (), s32[]{:S(2)}) async-start(), calls=%async_computation.3 | async-start | bytes 1253376 | tf_op jit(solution)/shard_map/all_gather | solution.py:81
  9.5 27.2 %all-to-all-start = ((s32[16,4,768]{2,1,0:T(4,128)}), s32[16,4,768]{2,1,0:T(4,128)S(1)}, u32[]{:S(2)}, u32[]{:S(2)}) async-start(s32[16,4,768]{2,1,0:T(4,128)} %broadcast_in_dim.28), calls=%async_computation | async-start | bytes 393216 | tf_op jit(solution)/shard_map/all_to_all | solution.py:22
  24.1 10.2 %copy-start.4 = (bf16[768]{0:T(1024)(128)(2,1)}, bf16[768]{0:T(1024)(128)(2,1)S(1)}, u32[]{:S(2)}) copy-start(bf16[768]{0:T(1024)(128)(2,1)S(1)} %select_convert_fusion.2) | copy-start | bytes 4612
  26.1 5.0 %copy-start.9 = (bf16[768]{0:T(1024)(128)(2,1)}, bf16[768]{0:T(1024)(128)(2,1)S(1)}, u32[]{:S(2)}) copy-start(bf16[768]{0:T(1024)(128)(2,1)S(1)} %get-tuple-element.20) | copy-start | bytes 4612
  26.2 4.9 %copy-start.6 = (s32[768]{0:T(1024)}, s32[768]{0:T(1024)S(1)}, u32[]{:S(2)}) copy-start(s32[768]{0:T(1024)S(1)} %dynamic-slice.2) | copy-start | bytes 9220
  31.1 1.1 copy-start.2
  31.1 3.3 %copy-start = (s32[48,768]{1,0:T(8,128)S(1)}, s32[48,768]{1,0:T(8,128)}, u32[]{:S(2)}) copy-start(s32[48,768]{1,0:T(8,128)} %param.3) | copy-start | bytes 442372
  36.6 1.1 copy-start.1
  37.8 20.8 %all-to-all-start.1 = ((s32[8,48,768]{2,1,0:T(8,128)}), s32[8,48,768]{2,1,0:T(8,128)S(1)}, u32[]{:S(2)}, u32[]{:S(2)}) async-start(s32[8,48,768]{2,1,0:T(8,128)} %broadcast_in_dim.32), calls=%async_computation.1 | async-start | bytes 2359296 | tf_op jit(solution)/shard_map/all_to_all | solution.py:22
  67.7 8.0 %copy-start.5 = (bf16[768]{0:T(1024)(128)(2,1)S(1)}, bf16[768]{0:T(1024)(128)(2,1)}, u32[]{:S(2)}) copy-start(bf16[768]{0:T(1024)(128)(2,1)} %copy-done.4) | copy-start | bytes 4612
  67.7 8.0 %copy-start.7 = (s32[768]{0:T(1024)S(1)}, s32[768]{0:T(1024)}, u32[]{:S(2)}) copy-start(s32[768]{0:T(1024)} %copy-done.6) | copy-start | bytes 9220
  67.7 8.0 %copy-start.10 = (bf16[768]{0:T(1024)(128)(2,1)S(1)}, bf16[768]{0:T(1024)(128)(2,1)}, u32[]{:S(2)}) copy-start(bf16[768]{0:T(1024)(128)(2,1)} %copy-done.9) | copy-start | bytes 4612
  67.8 8.0 %copy-start.11 = (f32[768]{0:T(1024)S(1)}, f32[768]{0:T(1024)}, u32[]{:S(2)}) copy-start(f32[768]{0:T(1024)} %get-tuple-element.19) | copy-start | bytes 9220
  75.8 20.7 %copy-start.3 = (f32[1536]{0:T(1024)S(1)}, f32[1536]{0:T(1024)}, u32[]{:S(2)}) copy-start(f32[1536]{0:T(1024)} %get-tuple-element.6) | copy-start | bytes 18436
  75.8 72.5 %copy-start.8 = (s32[256]{0:T(256)S(1)}, s32[256]{0:T(256)}, u32[]{:S(2)}) copy-start(s32[256]{0:T(256)} %param.5) | copy-start | bytes 3076
  98.3 50.1 %all-to-all-start.2 = ((f32[32,1,3072]{2,1,0:T(1,128)}), f32[32,1,3072]{2,1,0:T(1,128)S(1)}, u32[]{:S(2)}, u32[]{:S(2)}) async-start(f32[32,1,3072]{2,1,0:T(1,128)} %broadcast_in_dim.35), calls=%async_computation.2 | async-start | bytes 786432 | tf_op jit(solution)/shard_map/all_to_all | solution.py:22
Sparse Core Ops, SparseCore 0:
  9.8 56.5 all-gather.1
where the time goes:
time: 157 us; the launch traced here: 156 us
  blocking collectives  39.5 us (25%)
  other arithmetic  31.9 us (20%)
  starting transfers between devices  25.8 us (16%)
  matrix products  24 us (15%)
  between operations  13.7 us (9%)
  local copies, waits for them, and re-layouts  12.5 us (8%)
  waiting for transfers between devices  8.73 us (6%)
    psum x5, blocking collectives, by_axis(): value = lax.psum(value, axis)  39.5 us
    all_to_all x3, starting transfers between devices, from_everyone(): return lax.all_to_all(copies, axis, split_axis=0, concat_axis=0, tiled=True)  25.8 us
    dot_general x1, matrix products, body(): jnp.dot(row_slice, column_bits, preferred_element_type=jnp.float32)  20.7 us
    mul x1, other arithmetic, body(): column_bits = unpack(section) * keep_mid[:, None]  9.19 us
    all_to_all x3, waiting for transfers between devices, from_everyone(): return lax.all_to_all(copies, axis, split_axis=0, concat_axis=0, tiled=True)  8.7 us
    convert_element_type x1, other arithmetic, unpack(): bit_grid.reshape(packed.shape[0] * 32, packed.shape[1]).astype(jnp.bfloat16)  7.98 us
    reduce_or x3, other arithmetic, light_flags(): is_hub = jnp.any(vertex_ids[:, None] == hub_ids[None, :], axis=1)  4.72 us
    broadcast_in_dim x3, local copies, waits for them, and re-layouts, from_everyone(): copies = jnp.broadcast_to(value, (lax.axis_size(axis), *value.shape))  3.46 us
  transfers between devices with their start and end apart: 4, of which 1 were waited for; matrix products, arithmetic and copies ran while one was open for 23% of the time, Pallas kernels for 0%

commit v1 on v0

v1 whole, which is shorter than its diff:
```python
import functools

import jax
import jax.numpy as jnp
from jax import lax
from jax.experimental import pallas as pl
from jax.experimental.pallas import tpu as pltpu
from jax.sharding import PartitionSpec as P

MESH = pl.DeviceIdType.MESH
F32 = jnp.float32
F8 = jnp.float8_e4m3fn

THIRD = [
    0, 0, 47, 11, 19, 60, 25, 61, 42, 60, 37, 30, 41, 62, 26, 47,
    52, 16, 9, 9, 6, 34, 46, 19, 20, 46, 59, 37, 52, 19, 60, 48,
    1, 53, 11, 47, 18, 18, 29, 57, 53, 33, 13, 59, 6, 39, 41, 62,
    34, 6, 56, 12, 52, 16, 27, 27, 22, 4, 39, 40, 56, 52, 55, 13,
    14, 24, 25, 56, 56, 19, 43, 15, 36, 36, 57, 29, 50, 57, 15, 43,
    57, 2, 14, 2, 2, 38, 49, 26, 38, 2, 45, 45, 22, 4, 3, 62,
    19, 32, 56, 41, 43, 10, 13, 19, 5, 35, 25, 47, 54, 54, 47, 3,
    6, 12, 11, 21, 20, 24, 26, 32, 32, 22, 44, 10, 10, 38, 63, 63,
]


def destinations():
    rows, cols = [0] * 128, [0] * 128
    for i in range(8):
        for j in range(8):
            for h in range(2):
                for s in range(2):
                    k = THIRD[(i * 8 + j) * 2 + h] >> (3 * s) & 7
                    if i != j and k != j:
                        rows[(i * 8 + k) * 2 + h] |= 1 << (2 * j + s)
                    if i != j and k != i:
                        cols[(k * 8 + j) * 2 + h] |= 1 << (2 * i + s)
    return rows, cols


def lookup(tables, index, bits):
    tables = [list(t) for t in tables]
    for b in range(bits):
        bit = lax.rem(lax.div(index, 2**b), 2)
        for n, t in enumerate(tables):
            pairs = []
            for low, high in zip(t[0::2], t[1::2]):
                if isinstance(low, int) and isinstance(high, int) and low == high:
                    pairs.append(low)
                else:
                    pairs.append(low + bit * (high - low))
            tables[n] = pairs
    return [t[0] for t in tables]


def bit_of(mask, n):
    return lax.rem(lax.div(mask, lax.shift_left(jnp.int32(1), n)), 2) == 1


def rows_of_bits(words, first, count):
    shift = lax.broadcasted_iota(jnp.int32, (32, words.shape[1]), 0)
    spread = [jnp.broadcast_to(words[w : w + 1, :], shift.shape) for w in range(first, first + count)]
    return [jnp.bitwise_and(jnp.right_shift(x, shift), 1) for x in spread]


def unpack_into(dst, src, words, lane=0):
    width = src.shape[1]

    def step(g, carry):
        block = src[pl.ds(pl.multiple_of(g * 8, 8), 8), :]
        for n, bits in enumerate(rows_of_bits(block, 0, 8)):
            at = pl.multiple_of(g * 256 + n * 32, 32)
            dst[pl.ds(at, 32), lane : lane + width] = bits.astype(F32).astype(dst.dtype)
        return carry

    lax.fori_loop(0, words // 8, step, 0)


def kernel(
    lb, hb, ids_s, ids_v, out,
    m1, m2, m3, mm1, hubw, hub_i, a8, b8, o8, r8,
    acc_r, acc_c, col, col_in, hpart, h_in, segs, inbox,
    local_sem, send_sem, recv_sem, hub_send, hub_recv, ha_send, ha_recv, cs_sem, cr_sem, fs_sem, fr_sem,
):
    I = lax.axis_index("rows")
    c = lax.axis_index("cols")
    h = lax.axis_index("hub")
    J = lax.div(c, 2)
    s = lax.rem(c, 2)
    o = 1 - s
    W = m1.shape[1]
    C = m1.shape[2]
    B = 2 * C
    diag = I == J

    load_l = pltpu.make_async_copy(lb, m1.at[s], local_sem.at[0])
    load_h = pltpu.make_async_copy(hb, hubw, local_sem.at[1])
    load_l.start()
    load_h.start()

    barrier = pltpu.get_barrier_semaphore()

    def signal(dev):
        pl.semaphore_signal(barrier, inc=1, device_id=dev, device_id_type=MESH)

    def greet_plane(n, carry):
        @pl.when(n != c * 2 + h)
        def _():
            signal((I, lax.div(n, 2), lax.rem(n, 2)))

        return carry

    def greet_column(n, carry):
        @pl.when(lax.div(n, 2) != I)
        def _():
            signal((lax.div(n, 2), 2 * J + lax.rem(n, 2), h))

        return carry

    lax.fori_loop(0, 32, greet_plane, 0)
    lax.fori_loop(0, 16, greet_column, 0)

    to_rows, to_cols, thirds = lookup([ROWS_TO, COLS_TO, THIRD], (I * 8 + J) * 2 + h, 7)
    K = lax.rem(lax.div(thirds, 1 + 7 * s), 8)

    lane_w = lax.broadcasted_iota(jnp.int32, (8, 128), 1)
    sub_w = lax.broadcasted_iota(jnp.int32, (8, 128), 0)
    word_id = jnp.where(sub_w == 0, I * W, K * W) + lane_w
    word_id = jnp.where(lane_w < W, word_id, -1)
    col_id = J * B + lax.broadcasted_iota(jnp.int32, (16, 128), 0) * 128 + lax.broadcasted_iota(jnp.int32, (16, 128), 1)

    def mark(g, carry):
        words, flags = carry
        for n in range(16):
            v = ids_s[g * 16 + n]
            words = words | jnp.where(
                word_id == jnp.right_shift(v, 5), jnp.left_shift(jnp.int32(1), jnp.bitwise_and(v, 31)), 0
            )
            flags = flags | (col_id == v).astype(jnp.int32)
        return words, flags

    words, flags = lax.fori_loop(
        0, 16, mark, (jnp.zeros((8, 128), jnp.int32), jnp.zeros((16, 128), jnp.int32))
    )
    keep_words = jnp.bitwise_not(words)
    keep_i = jnp.broadcast_to(keep_words[0:1, :], (128, 128)).T[:W]
    keep_k = jnp.broadcast_to(keep_words[1:2, :], (128, 128)).T[:W]
    keep_col = flags - 1

    load_l.wait()
    load_h.wait()
    pl.semaphore_wait(barrier, 45)

    own = m1.at[s]

    def to_row(n):
        return pltpu.make_async_remote_copy(
            own, m2.at[s], send_sem.at[n], recv_sem.at[2 + s], device_id=(I, n, h), device_id_type=MESH
        )

    def to_col(n):
        return pltpu.make_async_remote_copy(
            own,
            m3.at[s],
            send_sem.at[16 + n],
            recv_sem.at[4 + s],
            device_id=(lax.div(n, 2), 2 * J + lax.rem(n, 2), h),
            device_id_type=MESH,
        )

    def to_twin():
        return pltpu.make_async_remote_copy(
            own, m1.at[s], send_sem.at[32], recv_sem.at[s], device_id=(I, c + 1 - 2 * s, h), device_id_type=MESH
        )

    def to_hub(n):
        return pltpu.make_async_remote_copy(
            hubw, hub_i.at[s], hub_send.at[n], hub_recv.at[s], device_id=(I, n, h), device_id_type=MESH
        )

    def each_hub(act):
        @pl.when(diag)
        def _():
            def step(n, carry):
                @pl.when(n != c)
                def _():
                    act(to_hub(n))

                return carry

            lax.fori_loop(0, 16, step, 0)

    def each_block(act):
        def step(n, carry):
            @pl.when(bit_of(to_cols, n))
            def _():
                act(to_col(n))

            @pl.when(bit_of(to_rows, n))
            def _():
                act(to_row(n))

            return carry

        lax.fori_loop(0, 16, step, 0)
        act(to_twin())

    each_hub(lambda d: d.start())
    each_block(lambda d: d.start())

    def mask_half(half):
        for t in range(C // 128):
            at = slice(t * 128, t * 128 + 128)
            lanes = keep_cols_of(half, t)
            mm1[half, :, at] = m1[half, :, at] & keep_i & lanes

    def keep_cols_of(half, t):
        if isinstance(half, int):
            return keep_col[half * (C // 128) + t : half * (C // 128) + t + 1, :]
        return jnp.where(half == 0, keep_col[t : t + 1, :], keep_col[C // 128 + t : C // 128 + t + 1, :])

    mask_half(s)
    unpack_into(o8, mm1.at[s], W)

    @pl.when(diag)
    def _():
        hub_i[s] = hubw[...]

    def hub_half(half):
        pltpu.make_async_copy(hubw, hub_i.at[half], hub_recv.at[half]).wait()

    @pl.when(jnp.logical_not(diag))
    def _():
        hub_half(s)

    hub_half(o)
    G = hubw.shape[0]
    for half in range(2):
        for n, bits in enumerate(rows_of_bits(hub_i[half], 0, G)):
            r8[n * 32 : n * 32 + 32, half * C : half * C + C] = bits.astype(F32).astype(F8)
    reach = jnp.dot(r8[...], o8[...], preferred_element_type=F32)
    edge = hubw[...]
    lanes_c = jnp.concatenate([keep_cols_of(s, t) for t in range(C // 128)], axis=1)
    edge = edge & lanes_c
    hub_bits = jnp.concatenate(rows_of_bits(edge, 0, G), axis=0)
    meet = jnp.where(hub_bits != 0, reach, 0.0)
    hub_flag = hub_bits.astype(F32)

    def across(x):
        t = x[:, 0:128]
        for n in range(1, x.shape[1] // 128):
            t = t + x[:, n * 128 : n * 128 + 128]
        return jnp.sum(t.T, axis=0, keepdims=True)

    hub_tri = 0.5 * across(meet)
    hub_deg = across(hub_flag)
    hpart[...] = hub_tri

    def to_column(n):
        return pltpu.make_async_remote_copy(
            hpart, h_in.at[I], ha_send.at[n], ha_recv.at[I], device_id=(n, c, h), device_id_type=MESH
        )

    def others(act):
        def step(n, carry):
            @pl.when(n != I)
            def _():
                act(n)

            return carry

        lax.fori_loop(0, 8, step, 0)

    others(lambda n: to_column(n).start())

    light_deg = jnp.sum(lax.population_count(mm1[s]).astype(F32), axis=0, keepdims=True) * 0.5
    edge_deg = jnp.sum(lax.population_count(edge).astype(F32), axis=0, keepdims=True)
    col_deg = light_deg + jnp.where(diag, 1.0, 0.0) * edge_deg
    col_tri = jnp.sum(meet, axis=0, keepdims=True)
    zero = jnp.zeros((1, C), F32)
    for half in range(2):
        here = s == half
        col[0:1, half * C : half * C + C] = jnp.where(here, col_tri, zero)
        col[1:2, half * C : half * C + C] = jnp.where(here, col_deg, zero)

    def recv(ref, sem):
        pltpu.make_async_copy(own, ref, sem).wait()

    recv(m1.at[o], recv_sem.at[o])
    mask_half(o)

    @pl.when(K != J)
    def _():
        recv(m2.at[0], recv_sem.at[2])
        recv(m2.at[1], recv_sem.at[3])

    @pl.when(K == J)
    def _():
        m2[...] = m1[...]

    unpack_into(a8, m2.at[0], W, 0)
    unpack_into(a8, m2.at[1], W, C)

    @pl.when(K != I)
    def _():
        recv(m3.at[0], recv_sem.at[4])
        recv(m3.at[1], recv_sem.at[5])

    @pl.when(K == I)
    def _():
        m3[...] = m1[...]

    for half in range(2):
        for t in range(C // 128):
            at = slice(t * 128, t * 128 + 128)
            m3[half, :, at] = m3[half, :, at] & keep_k
    unpack_into(b8, m3.at[0], W, 0)
    unpack_into(b8, m3.at[1], W, C)

    acc_r[...] = jnp.zeros_like(acc_r)
    MC, NC = 512, 256
    shift = lax.broadcasted_iota(jnp.int32, (32, NC), 0)

    for half in range(2):

        def chunk(n, carry, half=half):
            at = pl.multiple_of(n * NC, NC)
            sums = jnp.zeros((8, NC), F32)
            for m in range(B // MC):
                paths = jnp.dot(
                    a8[m * MC : m * MC + MC, :],
                    b8[:, pl.ds(pl.multiple_of(half * C + n * NC, NC), NC)],
                    preferred_element_type=F32,
                )
                for w in range(MC // 32):
                    word = m * (MC // 32) + w
                    x = jnp.broadcast_to(mm1[half, word : word + 1, pl.ds(at, NC)], (32, NC))
                    bits = jnp.bitwise_and(jnp.right_shift(x, shift), 1)
                    t = jnp.where(bits != 0, paths[w * 32 : w * 32 + 32], 0.0)
                    sums = sums + jnp.sum(t.reshape(4, 8, NC), axis=0)
                    acc_r[word * 32 : word * 32 + 32, :] += t[:, :128] + t[:, 128:]
            acc_c[:, pl.ds(pl.multiple_of(half * C + n * NC, NC), NC)] = sums
            return carry

        lax.fori_loop(0, C // NC, chunk, 0)

    row_w = jnp.where(diag, 0.125, jnp.where(K == I, 1.0, 0.5))
    col_w = jnp.where(diag, 0.0, jnp.where(K == J, 1.0, 0.5))
    col[0:1, :] += col_w * jnp.sum(acc_c[...], axis=0, keepdims=True)

    def to_diag():
        return pltpu.make_async_remote_copy(
            col, col_in.at[I], cs_sem, cr_sem.at[I], device_id=(J, c, h), device_id_type=MESH
        )

    @pl.when(jnp.logical_not(diag))
    def _():
        to_diag().start()

    def wait_hub(n):
        pltpu.make_async_copy(hpart, h_in.at[n], ha_recv.at[n]).wait()

    h_in[I] = hpart[...]
    others(wait_hub)
    hub_all = h_in[0]
    for n in range(1, 8):
        hub_all = hub_all + h_in[n]
    V = out.shape[1]
    pad = jnp.zeros((1, 128 - V), F32)
    for n in range(B // V):
        part = jnp.sum(acc_r[n * V : n * V + V, :].T, axis=0, keepdims=True) * row_w
        segs[n, 0:1, :] = jnp.concatenate([part, pad], axis=1)
        segs[n, 1:2, :] = jnp.zeros((1, 128), F32)
        segs[n, 2:3, :] = hub_all
        segs[n, 3:4, :] = hub_deg

    @pl.when(diag)
    def _():
        def wait_col(n):
            pltpu.make_async_copy(col, col_in.at[n], cr_sem.at[n]).wait()

        others(wait_col)
        col_in[I] = col[...]
        whole = col_in[0]
        for n in range(1, 8):
            whole = whole + col_in[n]
        for n in range(B // V):
            segs[n, 0:2, 0:V] += whole[:, n * V : n * V + V]

    me = c * 2 + h

    def to_plane(n):
        return pltpu.make_async_remote_copy(
            segs.at[lax.div(n, 2)],
            inbox.at[me],
            fs_sem.at[n],
            fr_sem.at[me],
            device_id=(I, lax.div(n, 2), lax.rem(n, 2)),
            device_id_type=MESH,
        )

    def plane(act):
        def step(n, carry):
            @pl.when(n != me)
            def _():
                act(n)

            return carry

        lax.fori_loop(0, 32, step, 0)

    plane(lambda n: to_plane(n).start())
    inbox[me] = segs[c]

    vertex = I * B + c * V + lax.broadcasted_iota(jnp.int32, (V, 128), 0)
    is_hub = [vertex == ids_v[g : g + 1, :] for g in range(2)]

    plane(lambda n: pltpu.make_async_copy(segs.at[0], inbox.at[n], fr_sem.at[n]).wait())
    even = inbox[0]
    odd = inbox[1]
    for n in range(1, 16):
        even = even + inbox[2 * n]
        odd = odd + inbox[2 * n + 1]
    both = even + odd

    def at_hubs(r):
        rows = [jnp.broadcast_to(x[r : r + 1, :], (V, 128)) for x in (even, odd)]
        hit = jnp.where(is_hub[0], rows[0], 0.0) + jnp.where(is_hub[1], rows[1], 0.0)
        return jnp.sum(hit.T, axis=0, keepdims=True)

    tri = both[0:1, :V] + at_hubs(2)
    deg = both[1:2, :V] + at_hubs(3)
    out[...] = tri / (1.0 + deg)

    each_hub(lambda d: d.wait_send())
    each_block(lambda d: d.wait_send())
    others(lambda n: to_column(n).wait_send())

    @pl.when(jnp.logical_not(diag))
    def _():
        to_diag().wait_send()

    plane(lambda n: to_plane(n).wait_send())


ROWS_TO, COLS_TO = destinations()


def body(light_bits, hub_bits, hub_ids):
    W, C = light_bits.shape
    G = hub_bits.shape[0]
    B = 2 * C
    V = B // 16
    vmem = pl.BlockSpec(memory_space=pltpu.VMEM)
    out = pl.pallas_call(
        kernel,
        out_shape=jax.ShapeDtypeStruct((1, V), F32),
        in_specs=[
            pl.BlockSpec(memory_space=pl.ANY),
            pl.BlockSpec(memory_space=pl.ANY),
            pl.BlockSpec(memory_space=pltpu.SMEM),
            vmem,
        ],
        out_specs=vmem,
        scratch_shapes=[
            pltpu.VMEM((2, W, C), jnp.int32),
            pltpu.VMEM((2, W, C), jnp.int32),
            pltpu.VMEM((2, W, C), jnp.int32),
            pltpu.VMEM((2, W, C), jnp.int32),
            pltpu.VMEM((G, C), jnp.int32),
            pltpu.VMEM((2, G, C), jnp.int32),
            pltpu.VMEM((B, B), F8),
            pltpu.VMEM((B, B), F8),
            pltpu.VMEM((B, C), F8),
            pltpu.VMEM((32 * G, B), F8),
            pltpu.VMEM((B, 128), F32),
            pltpu.VMEM((8, B), F32),
            pltpu.VMEM((2, B), F32),
            pltpu.VMEM((8, 2, B), F32),
            pltpu.VMEM((1, 128), F32),
            pltpu.VMEM((8, 1, 128), F32),
            pltpu.VMEM((16, 4, 128), F32),
            pltpu.VMEM((32, 4, 128), F32),
            pltpu.SemaphoreType.DMA((2,)),
            pltpu.SemaphoreType.DMA((33,)),
            pltpu.SemaphoreType.DMA((6,)),
            pltpu.SemaphoreType.DMA((16,)),
            pltpu.SemaphoreType.DMA((2,)),
            pltpu.SemaphoreType.DMA((8,)),
            pltpu.SemaphoreType.DMA((8,)),
            pltpu.SemaphoreType.DMA,
            pltpu.SemaphoreType.DMA((8,)),
            pltpu.SemaphoreType.DMA((32,)),
            pltpu.SemaphoreType.DMA((32,)),
        ],
        compiler_params=pltpu.CompilerParams(
            collective_id=0, has_side_effects=True, vmem_limit_bytes=48 * 2**20
        ),
    )(light_bits, hub_bits, hub_ids, hub_ids.reshape(2, 128))
    return out.reshape(V)


def solution(mesh):
    placed = (P("rows", "cols"), P("hub", "cols"), P())
    return jax.shard_map(body, mesh=mesh, in_specs=placed, out_specs=P(("rows", "cols")), check_vma=False)
```

time: 157 us -> 43 us (0.27)
  Pallas kernels: 0 us -> 40 us
  blocking collectives: 39.5 us -> 0 us
  other arithmetic: 31.9 us -> 0 us
  starting transfers between devices: 25.8 us -> 0 us
  matrix products: 24 us -> 0 us
  between operations: 13.7 us -> 0.01 us
  local copies, waits for them, and re-layouts: 12.5 us -> 2.81 us
  waiting for transfers between devices: 8.73 us -> 0 us
    pallas_call x0 -> x1, Pallas kernels: none -> 40 us  [body(): pl.pallas_call(kernel, out_shape=jax.ShapeDtypeStruct((1, V), F32), in_sp...]
    psum x5 -> x0, blocking collectives: 39.5 us -> none  [by_axis(): value = lax.psum(value, axis)]
    all_to_all x3 -> x0, starting transfers between devices: 25.8 us -> none  [from_everyone(): return lax.all_to_all(copies, axis, split_axis=0, concat_axis=0, tiled=True)]
    dot_general x2 -> x0, matrix products: 24 us -> none  [the longest x1 20.7 us: body(): jnp.dot(row_slice, column_bits, preferred_element_type=jnp.float32)]
    mul x6 -> x0, other arithmetic: 13.6 us -> none  [the longest x1 9.19 us: body(): column_bits = unpack(section) * keep_mid[:, None]]
    all_to_all x3 -> x0, waiting for transfers between devices: 8.7 us -> none  [from_everyone(): return lax.all_to_all(copies, axis, split_axis=0, concat_axis=0, tiled=True)]
    convert_element_type x5 -> x0, other arithmetic: 8.68 us -> none  [the longest x1 7.98 us: unpack(): bit_grid.reshape(packed.shape[0] * 32, packed.shape[1]).astype(jnp.bfloat16)]
    reduce_or x3 -> x0, other arithmetic: 4.72 us -> none  [light_flags(): is_hub = jnp.any(vertex_ids[:, None] == hub_ids[None, :], axis=1)]
  transfers between devices with their start and end apart: 4 -> 0, of which waited for: 1 -> 0; matrix products, arithmetic and copies ran while one was open for 23% -> 0% of each run, Pallas kernels for 0% -> 0%
where the time goes in v1:
time: 43 us; the launch traced here: 42.8 us
  Pallas kernels  40 us (93%)
  local copies, waits for them, and re-layouts  2.81 us (7%)
    pallas_call x1, Pallas kernels, body(): pl.pallas_call(kernel, out_shape=jax.ShapeDtypeStruct((1, V), F32), in_sp...  40 us
    unnamed x7, local copies, waits for them, and re-layouts  2.81 us

profile of v1, /device:TPU:8, one launch (start us, length us, event | category | flops | bytes accessed | tf_op | source)
XLA Modules:
  0.0 42.8 jit_solution(706957218381449897)
XLA Ops:
  0.0 0.0 copy-start.2
  0.0 0.7 %copy-done.2 = s32[256]{0:T(256)S(1)} copy-done((s32[256]{0:T(256)S(1)}, s32[256]{0:T(256)}, u32[]{:S(2)}) %copy-start.2) | copy-done | bytes 1048
  0.7 0.0 copy-start
  0.7 0.9 %copy-done = s32[48,768]{1,0:T(8,128)S(1)} copy-done((s32[48,768]{1,0:T(8,128)S(1)}, s32[48,768]{1,0:T(8,128)}, u32[]{:S(2)}) %copy-start) | copy-done | bytes 147480
  1.6 0.0 copy-start.1
  1.6 0.7 %copy-done.1 = s32[4,768]{1,0:T(4,128)S(1)} copy-done((s32[4,768]{1,0:T(4,128)S(1)}, s32[4,768]{1,0:T(4,128)}, u32[]{:S(2)}) %copy-start.1) | copy-done | bytes 12312
  2.3 40.0 %shard_map.37 = f32[1,96]{1,0:T(1,128)S(1)} custom-call(s32[48,768]{1,0:T(8,128)S(1)} %copy-done, s32[4,768]{1,0:T(4,128)S(1)} %copy-done.1, s32[256]{0:T(256)S(1)} %copy-done.2, s32[2,128]{1,0:T(2,128)S(1)} %bitcast.2), custom_call_target="tpu_custom_call" | custom-call | tf_op jit(solution)/shard_map/pallas_call | solution.py:454
  42.3 0.5 %copy.5 = f32[96]{0:T(128)} copy(f32[96]{0:T(128)S(1)} %bitcast.3) | data formatting | bytes 768
Async XLA Ops:
  0.0 0.7 %copy-start.2 = (s32[256]{0:T(256)S(1)}, s32[256]{0:T(256)}, u32[]{:S(2)}) copy-start(s32[256]{0:T(256)} %ids_s.1) | copy-start | bytes 3076
  0.7 0.9 %copy-start = (s32[48,768]{1,0:T(8,128)S(1)}, s32[48,768]{1,0:T(8,128)}, u32[]{:S(2)}) copy-start(s32[48,768]{1,0:T(8,128)} %lb.1) | copy-start | bytes 442372
  1.6 0.7 %copy-start.1 = (s32[4,768]{1,0:T(4,128)S(1)}, s32[4,768]{1,0:T(4,128)}, u32[]{:S(2)}) copy-start(s32[4,768]{1,0:T(4,128)} %hb.1) | copy-start | bytes 36868

commit v2 on v1

v2 whole, which is shorter than its diff:
```python
import functools

import jax
import jax.numpy as jnp
from jax import lax
from jax.experimental import pallas as pl
from jax.experimental.pallas import tpu as pltpu
from jax.sharding import PartitionSpec as P

MESH = pl.DeviceIdType.MESH
F32 = jnp.float32
F8 = jnp.float8_e4m3fn

THIRD = [
    0, 0, 47, 11, 19, 60, 25, 61, 42, 60, 37, 30, 41, 62, 26, 47,
    52, 16, 9, 9, 6, 34, 46, 19, 20, 46, 59, 37, 52, 19, 60, 48,
    1, 53, 11, 47, 18, 18, 29, 57, 53, 33, 13, 59, 6, 39, 41, 62,
    34, 6, 56, 12, 52, 16, 27, 27, 22, 4, 39, 40, 56, 52, 55, 13,
    14, 24, 25, 56, 56, 19, 43, 15, 36, 36, 57, 29, 50, 57, 15, 43,
    57, 2, 14, 2, 2, 38, 49, 26, 38, 2, 45, 45, 22, 4, 3, 62,
    19, 32, 56, 41, 43, 10, 13, 19, 5, 35, 25, 47, 54, 54, 47, 3,
    6, 12, 11, 21, 20, 24, 26, 32, 32, 22, 44, 10, 10, 38, 63, 63,
]


def destinations():
    rows, cols = [0] * 128, [0] * 128
    for i in range(8):
        for j in range(8):
            for h in range(2):
                for s in range(2):
                    k = THIRD[(i * 8 + j) * 2 + h] >> (3 * s) & 7
                    if i != j and k != j:
                        rows[(i * 8 + k) * 2 + h] |= 1 << (2 * j + s)
                    if i != j and k != i:
                        cols[(k * 8 + j) * 2 + h] |= 1 << (2 * i + s)
    return rows, cols


def lookup(tables, index, bits):
    tables = [list(t) for t in tables]
    for b in range(bits):
        odd = lax.rem(lax.div(index, 2**b), 2) == 1
        tables = [
            [x if isinstance(x, int) and x is y else jnp.where(odd, y, x) for x, y in zip(t[0::2], t[1::2])]
            for t in tables
        ]
    return [t[0] for t in tables]


def bit_of(mask, n):
    return lax.rem(lax.div(mask, 2**n), 2) == 1


def rows_of_bits(words, first, count):
    shift = lax.broadcasted_iota(jnp.int32, (32, words.shape[1]), 0)
    spread = [jnp.broadcast_to(words[w : w + 1, :], shift.shape) for w in range(first, first + count)]
    return [jnp.bitwise_and(jnp.right_shift(x, shift), 1) for x in spread]


def unpack_into(dst, src, words, lane=0):
    width = src.shape[1]

    def step(g, carry):
        block = src[pl.ds(pl.multiple_of(g * 8, 8), 8), :]
        for n, bits in enumerate(rows_of_bits(block, 0, 8)):
            at = pl.multiple_of(g * 256 + n * 32, 32)
            dst[pl.ds(at, 32), lane : lane + width] = bits.astype(F32).astype(dst.dtype)
        return carry

    lax.fori_loop(0, words // 8, step, 0)


def kernel(
    lb, hb, ids, out,
    ids_s, ids_v, m1, m2, m3, mm1, hubw, hub_i, a8, b8, o8, r8,
    acc_r, acc_c, col, hpart, h_in, rmsg, cmsg, r_in, c_in,
    local_sem, send_sem, recv_sem, hub_send, hub_recv, ha_send, ha_recv, rs_sem, rr_sem, cs_sem, cr_sem,
):
    I = lax.axis_index("rows")
    c = lax.axis_index("cols")
    h = lax.axis_index("hub")
    J = lax.div(c, 2)
    s = lax.rem(c, 2)
    o = 1 - s
    W = m1.shape[1]
    C = m1.shape[2]
    B = 2 * C
    V = out.shape[1]
    diag = I == J
    off = jnp.logical_not(diag)

    loads = [
        pltpu.make_async_copy(lb, m1.at[s], local_sem.at[0]),
        pltpu.make_async_copy(hb, hubw, local_sem.at[1]),
        pltpu.make_async_copy(ids, ids_s, local_sem.at[2]),
        pltpu.make_async_copy(ids, ids_v, local_sem.at[3]),
    ]
    for load in loads:
        load.start()

    barrier = pltpu.get_barrier_semaphore()

    def signal(dev):
        pl.semaphore_signal(barrier, inc=1, device_id=dev, device_id_type=MESH)

    me = c * 2 + h
    for n in range(1, 32):
        peer = lax.rem(me + n, 32)
        signal((I, lax.div(peer, 2), lax.rem(peer, 2)))
    for n in range(1, 8):
        for half in range(2):
            signal((lax.rem(I + n, 8), 2 * J + half, h))

    to_rows, to_cols, thirds = lookup([ROWS_TO, COLS_TO, THIRD], (I * 8 + J) * 2 + h, 7)
    K = lax.rem(jnp.where(s == 1, lax.div(thirds, 8), thirds), 8)
    loads[0].wait()
    loads[1].wait()
    pl.semaphore_wait(barrier, 45)

    own = m1.at[s]

    def to_row(n):
        return pltpu.make_async_remote_copy(
            own, m2.at[s], send_sem.at[n], recv_sem.at[2 + s], device_id=(I, n, h), device_id_type=MESH
        )

    def to_col(n):
        return pltpu.make_async_remote_copy(
            own,
            m3.at[s],
            send_sem.at[16 + n],
            recv_sem.at[4 + s],
            device_id=(n // 2, 2 * J + n % 2, h),
            device_id_type=MESH,
        )

    def to_twin():
        return pltpu.make_async_remote_copy(
            own, m1.at[s], send_sem.at[32], recv_sem.at[s], device_id=(I, c + 1 - 2 * s, h), device_id_type=MESH
        )

    def to_hub(n):
        return pltpu.make_async_remote_copy(
            hubw, hub_i.at[s], hub_send.at[n], hub_recv.at[s], device_id=(I, n, h), device_id_type=MESH
        )

    def each_hub(act):
        @pl.when(diag)
        def _():
            for n in range(16):
                @pl.when(n != c)
                def _(n=n):
                    act(to_hub(n))

    def each_block(act):
        for n in range(16):
            @pl.when(bit_of(to_rows, n))
            def _(n=n):
                act(to_row(n))

        for n in range(16):
            @pl.when(bit_of(to_cols, n))
            def _(n=n):
                act(to_col(n))

        act(to_twin())

    each_hub(lambda d: d.start())
    each_block(lambda d: d.start())

    loads[2].wait()
    loads[3].wait()
    lane_w = lax.broadcasted_iota(jnp.int32, (8, 128), 1)
    sub_w = lax.broadcasted_iota(jnp.int32, (8, 128), 0)
    word_id = jnp.where(sub_w == 0, I * W, K * W) + lane_w
    word_id = jnp.where(lane_w < W, word_id, -1)
    col_id = J * B + lax.broadcasted_iota(jnp.int32, (16, 128), 0) * 128 + lax.broadcasted_iota(jnp.int32, (16, 128), 1)

    def mark(g, carry):
        words, flags = carry
        for n in range(16):
            v = ids_s[lax.div(g, 8), lax.rem(g, 8) * 16 + n]
            words = words | jnp.where(
                word_id == jnp.right_shift(v, 5), jnp.left_shift(jnp.int32(1), jnp.bitwise_and(v, 31)), 0
            )
            flags = flags | (col_id == v).astype(jnp.int32)
        return words, flags

    words, flags = lax.fori_loop(
        0, 16, mark, (jnp.zeros((8, 128), jnp.int32), jnp.zeros((16, 128), jnp.int32))
    )
    keep_words = jnp.bitwise_not(words)
    keep_i = jnp.broadcast_to(keep_words[0:1, :], (128, 128)).T[:W]
    keep_k = jnp.broadcast_to(keep_words[1:2, :], (128, 128)).T[:W]
    keep_col = flags - 1

    def keep_cols_of(half, t):
        n = C // 128
        return jnp.where(half == 0, keep_col[t : t + 1, :], keep_col[n + t : n + t + 1, :])

    def mask_half(half):
        for t in range(C // 128):
            at = slice(t * 128, t * 128 + 128)
            mm1[half, :, at] = m1[half, :, at] & keep_i & keep_cols_of(half, t)

    mask_half(s)
    unpack_into(o8, mm1.at[s], W)

    @pl.when(diag)
    def _():
        hub_i[s] = hubw[...]

    def hub_half(half):
        pltpu.make_async_copy(hubw, hub_i.at[half], hub_recv.at[half]).wait()

    @pl.when(off)
    def _():
        hub_half(s)

    hub_half(o)
    G = hubw.shape[0]
    for half in range(2):
        for n, bits in enumerate(rows_of_bits(hub_i[half], 0, G)):
            r8[n * 32 : n * 32 + 32, half * C : half * C + C] = bits.astype(F32).astype(F8)
    reach = jnp.dot(r8[...], o8[...], preferred_element_type=F32)
    edge = hubw[...]
    lanes_c = jnp.concatenate([keep_cols_of(s, t) for t in range(C // 128)], axis=1)
    edge = edge & lanes_c
    hub_bits = jnp.concatenate(rows_of_bits(edge, 0, G), axis=0)
    meet = jnp.where(hub_bits != 0, reach, 0.0)
    hub_flag = hub_bits.astype(F32)

    def across(x):
        t = x[:, 0:128]
        for n in range(1, x.shape[1] // 128):
            t = t + x[:, n * 128 : n * 128 + 128]
        return jnp.sum(t.T, axis=0, keepdims=True)

    hub_tri = 0.5 * across(meet)
    hub_deg = across(hub_flag)
    hpart[...] = hub_tri

    def to_column(n):
        return pltpu.make_async_remote_copy(
            hpart, h_in.at[I], ha_send.at[n], ha_recv.at[I], device_id=(n, c, h), device_id_type=MESH
        )

    def others(act):
        for n in range(8):
            @pl.when(n != I)
            def _(n=n):
                act(n)

    others(lambda n: to_column(n).start())

    light_deg = jnp.sum(lax.population_count(mm1[s]).astype(F32), axis=0, keepdims=True) * 0.5
    edge_deg = jnp.sum(lax.population_count(edge).astype(F32), axis=0, keepdims=True)
    col[0:1, :] = jnp.sum(meet, axis=0, keepdims=True)
    col[1:2, :] = light_deg + jnp.where(diag, 1.0, 0.0) * edge_deg

    def recv(ref, sem):
        pltpu.make_async_copy(own, ref, sem).wait()

    @pl.when(K != J)
    def _():
        recv(m2.at[0], recv_sem.at[2])
        recv(m2.at[1], recv_sem.at[3])

    @pl.when(K == J)
    def _():
        recv(m1.at[o], recv_sem.at[o])
        m2[...] = m1[...]

    unpack_into(a8, m2.at[0], W, 0)
    unpack_into(a8, m2.at[1], W, C)
    acc_r[...] = jnp.zeros_like(acc_r)
    row_w = jnp.where(diag, 0.125, jnp.where(K == I, 1.0, 0.5))
    col_w = jnp.where(diag, 0.0, jnp.where(K == J, 1.0, 0.5))
    MC, NC = 512, 256
    shift = lax.broadcasted_iota(jnp.int32, (32, NC), 0)

    def to_owner(n, k):
        return pltpu.make_async_remote_copy(
            cmsg.at[n],
            c_in.at[I * 4 + s * 2 + h],
            cs_sem.at[n * 2 + k],
            cr_sem.at[I * 4 + s * 2 + h],
            device_id=(J, n, k),
            device_id_type=MESH,
        )

    def face(half, name):
        @pl.when(K != I)
        def _():
            recv(m3.at[half], recv_sem.at[4 + half])

        @pl.when(K == I)
        def _():
            m3[half] = m1[half]

        for t in range(C // 128):
            at = slice(t * 128, t * 128 + 128)
            m3[half, :, at] = m3[half, :, at] & keep_k
        unpack_into(b8.at[half], m3.at[half], W)

        def chunk(n, carry):
            at = pl.multiple_of(n * NC, NC)
            sums = jnp.zeros((8, NC), F32)
            for m in range(B // MC):
                paths = jnp.dot(
                    a8[m * MC : m * MC + MC, :], b8[half, :, pl.ds(at, NC)], preferred_element_type=F32
                )
                for w in range(MC // 32):
                    word = m * (MC // 32) + w
                    x = jnp.broadcast_to(mm1[half, word : word + 1, pl.ds(at, NC)], (32, NC))
                    bits = jnp.bitwise_and(jnp.right_shift(x, shift), 1)
                    t = jnp.where(bits != 0, paths[w * 32 : w * 32 + 32], 0.0)
                    sums = sums + jnp.sum(t.reshape(4, 8, NC), axis=0)
                    acc_r[word * 32 : word * 32 + 32, :] += t[:, :128] + t[:, 128:]
            acc_c[:, pl.ds(at, NC)] = sums
            return carry

        lax.fori_loop(0, C // NC, chunk, 0)

    def send_cols(half, first):
        whole = col_w * jnp.sum(acc_c[...], axis=0, keepdims=True)
        if first:
            whole = whole + col[0:1, :]
        for k in range(C // V):
            n = half * (C // V) + k
            cmsg[n, 0:1, 0:V] = whole[:, k * V : k * V + V]
            if first:
                cmsg[n, 1:2, 0:V] = col[1:2, k * V : k * V + V]
            else:
                cmsg[n, 1:2, 0:V] = jnp.zeros((1, V), F32)
        for k in range(C // V):
            n = half * (C // V) + k
            for g in range(2):
                @pl.when(jnp.logical_or(off, jnp.logical_or(n != c, g != h)))
                def _(n=n, g=g):
                    to_owner(n, g).start()

    face(s, "p13")
    others(lambda n: pltpu.make_async_copy(hpart, h_in.at[n], ha_recv.at[n]).wait())
    h_in[I] = hpart[...]
    send_cols(s, True)
    @pl.when(K != J)
    def _():
        recv(m1.at[o], recv_sem.at[o])

    mask_half(o)
    face(o, "p16")
    send_cols(o, False)

    hub_all = h_in[0]
    for n in range(1, 8):
        hub_all = hub_all + h_in[n]
    for n in range(B // V):
        rmsg[n, 0:1, 0:V] = jnp.sum(acc_r[n * V : n * V + V, :].T, axis=0, keepdims=True) * row_w
        rmsg[n, 1:2, :] = hub_all
        rmsg[n, 2:3, :] = hub_deg

    def to_plane(n):
        return pltpu.make_async_remote_copy(
            rmsg.at[n // 2],
            r_in.at[me],
            rs_sem.at[n],
            rr_sem.at[me],
            device_id=(I, n // 2, n % 2),
            device_id_type=MESH,
        )

    def plane(act):
        for n in range(32):
            @pl.when(n != me)
            def _(n=n):
                act(n)

    plane(lambda n: to_plane(n).start())
    r_in[me] = rmsg[c]

    @pl.when(diag)
    def _():
        c_in[I * 4 + s * 2 + h] = cmsg[c]

    vertex = I * B + c * V + lax.broadcasted_iota(jnp.int32, (V, 128), 0)
    is_hub = [vertex == ids_v[g : g + 1, :] for g in range(2)]
    each_hub(lambda d: d.wait_send())
    each_block(lambda d: d.wait_send())
    others(lambda n: to_column(n).wait_send())

    def wait_cols(n):
        pltpu.make_async_copy(cmsg.at[0], c_in.at[n], cr_sem.at[n]).wait()

    for n in range(32):
        @pl.when(jnp.logical_or(off, n != I * 4 + s * 2 + h))
        def _(n=n):
            wait_cols(n)

    plane(lambda n: pltpu.make_async_copy(rmsg.at[0], r_in.at[n], rr_sem.at[n]).wait())
    even = r_in[0]
    odd = r_in[1]
    for n in range(1, 16):
        even = even + r_in[2 * n]
        odd = odd + r_in[2 * n + 1]
    both = even + odd
    cols = c_in[0]
    for n in range(1, 32):
        cols = cols + c_in[n]

    def at_hubs(r):
        rows = [jnp.broadcast_to(x[r : r + 1, :], (V, 128)) for x in (even, odd)]
        hit = jnp.where(is_hub[0], rows[0], 0.0) + jnp.where(is_hub[1], rows[1], 0.0)
        return jnp.sum(hit.T, axis=0, keepdims=True)

    tri = both[0:1, :V] + cols[0:1, :V] + at_hubs(1)
    deg = cols[1:2, :V] + at_hubs(2)
    out[...] = tri / (1.0 + deg)
    for n in range(B // V):
        for g in range(2):
            @pl.when(jnp.logical_or(off, jnp.logical_or(n != c, g != h)))
            def _(n=n, g=g):
                to_owner(n, g).wait_send()

    plane(lambda n: to_plane(n).wait_send())


ROWS_TO, COLS_TO = destinations()


def body(light_bits, hub_bits, hub_ids):
    W, C = light_bits.shape
    G = hub_bits.shape[0]
    B = 2 * C
    V = B // 16
    vmem = pl.BlockSpec(memory_space=pltpu.VMEM)
    out = pl.pallas_call(
        kernel,
        out_shape=jax.ShapeDtypeStruct((1, V), F32),
        in_specs=[pl.BlockSpec(memory_space=pltpu.HBM)] * 3,
        out_specs=vmem,
        scratch_shapes=[
            pltpu.SMEM((2, 128), jnp.int32),
            pltpu.VMEM((2, 128), jnp.int32),
            pltpu.VMEM((2, W, C), jnp.int32),
            pltpu.VMEM((2, W, C), jnp.int32),
            pltpu.VMEM((2, W, C), jnp.int32),
            pltpu.VMEM((2, W, C), jnp.int32),
            pltpu.VMEM((G, C), jnp.int32),
            pltpu.VMEM((2, G, C), jnp.int32),
            pltpu.VMEM((B, B), F8),
            pltpu.VMEM((2, B, C), F8),
            pltpu.VMEM((B, C), F8),
            pltpu.VMEM((32 * G, B), F8),
            pltpu.VMEM((B, 128), F32),
            pltpu.VMEM((8, C), F32),
            pltpu.VMEM((2, C), F32),
            pltpu.VMEM((1, 128), F32),
            pltpu.VMEM((8, 1, 128), F32),
            pltpu.VMEM((16, 4, 128), F32),
            pltpu.VMEM((16, 2, 128), F32),
            pltpu.VMEM((32, 4, 128), F32),
            pltpu.VMEM((32, 2, 128), F32),
            pltpu.SemaphoreType.DMA((4,)),
            pltpu.SemaphoreType.DMA((33,)),
            pltpu.SemaphoreType.DMA((6,)),
            pltpu.SemaphoreType.DMA((16,)),
            pltpu.SemaphoreType.DMA((2,)),
            pltpu.SemaphoreType.DMA((8,)),
            pltpu.SemaphoreType.DMA((8,)),
            pltpu.SemaphoreType.DMA((32,)),
            pltpu.SemaphoreType.DMA((32,)),
            pltpu.SemaphoreType.DMA((32,)),
            pltpu.SemaphoreType.DMA((32,)),
        ],
        compiler_params=pltpu.CompilerParams(
            collective_id=0, has_side_effects=True, vmem_limit_bytes=67043328
        ),
    )(light_bits, hub_bits, hub_ids.reshape(2, 128))
    return out.reshape(V)


def solution(mesh):
    placed = (P("rows", "cols"), P("hub", "cols"), P())
    return jax.shard_map(body, mesh=mesh, in_specs=placed, out_specs=P(("rows", "cols")), check_vma=False)
```

time: 43 us -> 39.4 us (0.916)
  the two profiles are of different devices: /device:TPU:8 before, /device:TPU:24 now
where the time goes in v2:
time: 39.4 us; the launch traced here: 39.3 us
  Pallas kernels  38.2 us (97%)
  local copies, waits for them, and re-layouts  1.1 us (3%)
    pallas_call x1, Pallas kernels, body(): pl.pallas_call(kernel, out_shape=jax.ShapeDtypeStruct((1, V), F32), in_sp...  38.2 us
    unnamed x3, local copies, waits for them, and re-layouts  1.1 us

profile of v2, /device:TPU:24, one launch (start us, length us, event | category | flops | bytes accessed | tf_op | source)
XLA Modules:
  0.0 39.3 jit_solution(9518107588263602031)
XLA Ops:
  0.0 38.2 %shard_map.37 = f32[1,96]{1,0:T(1,128)} custom-call(s32[48,768]{1,0:T(8,128)} %lb.1, s32[4,768]{1,0:T(4,128)} %hb.1, s32[2,128]{1,0:T(2,128)} %bitcast.2), custom_call_target="tpu_custom_call" | custom-call | tf_op jit(solution)/shard_map/pallas_call | solution.py:438
  38.2 0.0 copy-start
  38.2 0.6 %copy-done = f32[1,96]{1,0:T(1,128)S(1)} copy-done((f32[1,96]{1,0:T(1,128)S(1)}, f32[1,96]{1,0:T(1,128)}, u32[]{:S(2)}) %copy-start) | copy-done | bytes 408
  38.8 0.5 %copy.5 = f32[96]{0:T(128)} copy(f32[96]{0:T(128)S(1)} %bitcast.3) | data formatting | bytes 768
Async XLA Ops:
  38.2 0.6 %copy-start = (f32[1,96]{1,0:T(1,128)S(1)}, f32[1,96]{1,0:T(1,128)}, u32[]{:S(2)}) copy-start(f32[1,96]{1,0:T(1,128)} %shard_map.37) | copy-start | bytes 1156

commit v3 on v2

--- a/solution.py
+++ b/solution.py
@@ -12,29 +12,39 @@
 F8 = jnp.float8_e4m3fn
 
 THIRD = [
-    0, 0, 47, 11, 19, 60, 25, 61, 42, 60, 37, 30, 41, 62, 26, 47,
-    52, 16, 9, 9, 6, 34, 46, 19, 20, 46, 59, 37, 52, 19, 60, 48,
-    1, 53, 11, 47, 18, 18, 29, 57, 53, 33, 13, 59, 6, 39, 41, 62,
-    34, 6, 56, 12, 52, 16, 27, 27, 22, 4, 39, 40, 56, 52, 55, 13,
-    14, 24, 25, 56, 56, 19, 43, 15, 36, 36, 57, 29, 50, 57, 15, 43,
-    57, 2, 14, 2, 2, 38, 49, 26, 38, 2, 45, 45, 22, 4, 3, 62,
-    19, 32, 56, 41, 43, 10, 13, 19, 5, 35, 25, 47, 54, 54, 47, 3,
-    6, 12, 11, 21, 20, 24, 26, 32, 32, 22, 44, 10, 10, 38, 63, 63,
+    0, 0, 47, 3, 42, 35, 59, 41, 28, 46, 60, 43, 52, 59, 46, 23,
+    52, 17, 9, 9, 22, 4, 37, 26, 53, 34, 47, 20, 39, 22, 53, 59,
+    62, 1, 11, 47, 18, 18, 17, 61, 4, 61, 33, 47, 48, 15, 37, 55,
+    48, 20, 62, 1, 3, 38, 27, 27, 40, 52, 13, 52, 47, 52, 14, 56,
+    15, 2, 25, 7, 11, 22, 11, 23, 36, 36, 25, 60, 62, 1, 59, 41,
+    16, 49, 48, 11, 16, 51, 24, 58, 2, 46, 45, 45, 20, 48, 14, 7,
+    13, 2, 13, 24, 35, 21, 1, 19, 42, 35, 43, 57, 54, 54, 46, 11,
+    32, 25, 32, 17, 8, 26, 26, 44, 22, 4, 26, 44, 60, 16, 63, 63,
 ]
 
 
+def nearer(j, k, h):
+    here = j // 2 * 2 + h
+
+    def hops(g):
+        d = (k // 2 * 2 + g - here) % 8
+        return min(d, 8 - d)
+
+    return 1 - h if hops(1 - h) < hops(h) else h
+
+
 def destinations():
-    rows, cols = [0] * 128, [0] * 128
+    rows, cols = ([0] * 128, [0] * 128), [0] * 128
     for i in range(8):
         for j in range(8):
             for h in range(2):
                 for s in range(2):
                     k = THIRD[(i * 8 + j) * 2 + h] >> (3 * s) & 7
                     if i != j and k != j:
-                        rows[(i * 8 + k) * 2 + h] |= 1 << (2 * j + s)
+                        rows[h][(i * 8 + k) * 2 + nearer(j, k, h)] |= 1 << (2 * j + s)
                     if i != j and k != i:
                         cols[(k * 8 + j) * 2 + h] |= 1 << (2 * i + s)
-    return rows, cols
+    return rows[0], rows[1], cols
 
 
 def lookup(tables, index, bits):
@@ -112,24 +122,25 @@
         for half in range(2):
             signal((lax.rem(I + n, 8), 2 * J + half, h))
 
-    to_rows, to_cols, thirds = lookup([ROWS_TO, COLS_TO, THIRD], (I * 8 + J) * 2 + h, 7)
+    to_rows0, to_rows1, to_cols, thirds = lookup([ROWS0_TO, ROWS1_TO, COLS_TO, THIRD], (I * 8 + J) * 2 + h, 7)
     K = lax.rem(jnp.where(s == 1, lax.div(thirds, 8), thirds), 8)
+    K_twin = lax.rem(jnp.where(s == 0, lax.div(thirds, 8), thirds), 8)
     loads[0].wait()
     loads[1].wait()
     pl.semaphore_wait(barrier, 45)
 
     own = m1.at[s]
 
-    def to_row(n):
-        return pltpu.make_async_remote_copy(
-            own, m2.at[s], send_sem.at[n], recv_sem.at[2 + s], device_id=(I, n, h), device_id_type=MESH
-        )
-
-    def to_col(n):
+    def to_row(n, g, sem):
+        return pltpu.make_async_remote_copy(
+            own, m2.at[s], send_sem.at[sem], recv_sem.at[2 + s], device_id=(I, n, g), device_id_type=MESH
+        )
+
+    def to_col(n, sem):
         return pltpu.make_async_remote_copy(
             own,
             m3.at[s],
-            send_sem.at[16 + n],
+            send_sem.at[sem],
             recv_sem.at[4 + s],
             device_id=(n // 2, 2 * J + n % 2, h),
             device_id_type=MESH,
@@ -137,7 +148,7 @@
 
     def to_twin():
         return pltpu.make_async_remote_copy(
-            own, m1.at[s], send_sem.at[32], recv_sem.at[s], device_id=(I, c + 1 - 2 * s, h), device_id_type=MESH
+            own, m1.at[s], send_sem.at[0], recv_sem.at[s], device_id=(I, c + 1 - 2 * s, h), device_id_type=MESH
         )
 
     def to_hub(n):
@@ -153,21 +164,30 @@
                 def _(n=n):
                     act(to_hub(n))
 
-    def each_block(act):
+    each_hub(lambda d: d.start())
+    sent = jnp.int32(1)
+    for g, mask in enumerate((to_rows0, to_rows1)):
         for n in range(16):
-            @pl.when(bit_of(to_rows, n))
-            def _(n=n):
-                act(to_row(n))
-
-        for n in range(16):
-            @pl.when(bit_of(to_cols, n))
-            def _(n=n):
-                act(to_col(n))
-
-        act(to_twin())
-
-    each_hub(lambda d: d.start())
-    each_block(lambda d: d.start())
+            go = bit_of(mask, n)
+
+            @pl.when(go)
+            def _(n=n, g=g, sent=sent):
+                to_row(n, g, sent).start()
+
+            sent = sent + go.astype(jnp.int32)
+
+    for n in range(16):
+        go = jnp.logical_and(bit_of(to_cols, n), s == n % 2)
+
+        @pl.when(go)
+        def _(n=n, sent=sent):
+            to_col(n, sent).start()
+
+        sent = sent + go.astype(jnp.int32)
+
+    @pl.when(K_twin == J)
+    def _():
+        to_twin().start()
 
     loads[2].wait()
     loads[3].wait()
@@ -243,7 +263,7 @@
 
     def to_column(n):
         return pltpu.make_async_remote_copy(
-            hpart, h_in.at[I], ha_send.at[n], ha_recv.at[I], device_id=(n, c, h), device_id_type=MESH
+            hpart, h_in.at[I], ha_send, ha_recv, device_id=(n, c, h), device_id_type=MESH
         )
 
     def others(act):
@@ -262,10 +282,22 @@
     def recv(ref, sem):
         pltpu.make_async_copy(own, ref, sem).wait()
 
+    for n in range(16):
+        go = jnp.logical_and(bit_of(to_cols, n), s != n % 2)
+
+        @pl.when(go)
+        def _(n=n, sent=sent):
+            to_col(n, sent).start()
+
+        sent = sent + go.astype(jnp.int32)
+
+    @pl.when(K_twin != J)
+    def _():
+        to_twin().start()
+
     @pl.when(K != J)
     def _():
         recv(m2.at[0], recv_sem.at[2])
-        recv(m2.at[1], recv_sem.at[3])
 
     @pl.when(K == J)
     def _():
@@ -273,19 +305,23 @@
         m2[...] = m1[...]
 
     unpack_into(a8, m2.at[0], W, 0)
+    @pl.when(K != J)
+    def _():
+        recv(m2.at[1], recv_sem.at[3])
+
     unpack_into(a8, m2.at[1], W, C)
     acc_r[...] = jnp.zeros_like(acc_r)
     row_w = jnp.where(diag, 0.125, jnp.where(K == I, 1.0, 0.5))
     col_w = jnp.where(diag, 0.0, jnp.where(K == J, 1.0, 0.5))
-    MC, NC = 512, 256
-    shift = lax.broadcasted_iota(jnp.int32, (32, NC), 0)
+    MC = 256
+    shift = lax.broadcasted_iota(jnp.int32, (32, C), 0)
 
     def to_owner(n, k):
         return pltpu.make_async_remote_copy(
             cmsg.at[n],
             c_in.at[I * 4 + s * 2 + h],
-            cs_sem.at[n * 2 + k],
-            cr_sem.at[I * 4 + s * 2 + h],
+            cs_sem,
+            cr_sem,
             device_id=(J, n, k),
             device_id_type=MESH,
         )
@@ -304,24 +340,29 @@
             m3[half, :, at] = m3[half, :, at] & keep_k
         unpack_into(b8.at[half], m3.at[half], W)
 
-        def chunk(n, carry):
-            at = pl.multiple_of(n * NC, NC)
-            sums = jnp.zeros((8, NC), F32)
-            for m in range(B // MC):
+        acc_c[...] = jnp.zeros_like(acc_c)
+
+        def chunk(g, carry):
+            sums = acc_c[...]
+            for u in range(2):
+                m = g * 2 + u
                 paths = jnp.dot(
-                    a8[m * MC : m * MC + MC, :], b8[half, :, pl.ds(at, NC)], preferred_element_type=F32
+                    a8[pl.ds(pl.multiple_of(m * MC, MC), MC), :], b8[half], preferred_element_type=F32
                 )
+                words = mm1[half, pl.ds(pl.multiple_of(m * (MC // 32), MC // 32), MC // 32), :]
                 for w in range(MC // 32):
-                    word = m * (MC // 32) + w
-                    x = jnp.broadcast_to(mm1[half, word : word + 1, pl.ds(at, NC)], (32, NC))
+                    x = jnp.broadcast_to(words[w : w + 1, :], (32, C))
                     bits = jnp.bitwise_and(jnp.right_shift(x, shift), 1)
                     t = jnp.where(bits != 0, paths[w * 32 : w * 32 + 32], 0.0)
-                    sums = sums + jnp.sum(t.reshape(4, 8, NC), axis=0)
-                    acc_r[word * 32 : word * 32 + 32, :] += t[:, :128] + t[:, 128:]
-            acc_c[:, pl.ds(at, NC)] = sums
+                    sums = sums + jnp.sum(t.reshape(4, 8, C), axis=0)
+                    row = t[:, 0:128]
+                    for q in range(1, C // 128):
+                        row = row + t[:, q * 128 : q * 128 + 128]
+                    acc_r[pl.ds(pl.multiple_of(m * MC + w * 32, 32), 32), :] += row
+            acc_c[...] = sums
             return carry
 
-        lax.fori_loop(0, C // NC, chunk, 0)
+        lax.fori_loop(0, B // (2 * MC), chunk, 0)
 
     def send_cols(half, first):
         whole = col_w * jnp.sum(acc_c[...], axis=0, keepdims=True)
@@ -342,7 +383,7 @@
                     to_owner(n, g).start()
 
     face(s, "p13")
-    others(lambda n: pltpu.make_async_copy(hpart, h_in.at[n], ha_recv.at[n]).wait())
+    pltpu.make_async_copy(h_in.at[pl.ds(0, 7)], h_in.at[pl.ds(0, 7)], ha_recv).wait()
     h_in[I] = hpart[...]
     send_cols(s, True)
     @pl.when(K != J)
@@ -365,8 +406,8 @@
         return pltpu.make_async_remote_copy(
             rmsg.at[n // 2],
             r_in.at[me],
-            rs_sem.at[n],
-            rr_sem.at[me],
+            rs_sem,
+            rr_sem,
             device_id=(I, n // 2, n % 2),
             device_id_type=MESH,
         )
@@ -387,18 +428,28 @@
     vertex = I * B + c * V + lax.broadcasted_iota(jnp.int32, (V, 128), 0)
     is_hub = [vertex == ids_v[g : g + 1, :] for g in range(2)]
     each_hub(lambda d: d.wait_send())
-    each_block(lambda d: d.wait_send())
-    others(lambda n: to_column(n).wait_send())
-
-    def wait_cols(n):
-        pltpu.make_async_copy(cmsg.at[0], c_in.at[n], cr_sem.at[n]).wait()
-
-    for n in range(32):
-        @pl.when(jnp.logical_or(off, n != I * 4 + s * 2 + h))
+    for n in range(MOST_SENDS):
+        @pl.when(n < sent)
         def _(n=n):
-            wait_cols(n)
-
-    plane(lambda n: pltpu.make_async_copy(rmsg.at[0], r_in.at[n], rr_sem.at[n]).wait())
+            pltpu.make_async_copy(own, m2.at[s], send_sem.at[n]).wait()
+
+    pltpu.make_async_copy(h_in.at[pl.ds(0, 7)], h_in.at[pl.ds(0, 7)], ha_send).wait()
+
+    def wait_slots(ref, sem, count):
+        part = ref.at[pl.ds(0, count)]
+        pltpu.make_async_copy(part, part, sem).wait()
+
+    def wait_cols(sem):
+        @pl.when(off)
+        def _():
+            wait_slots(c_in, sem, 32)
+
+        @pl.when(diag)
+        def _():
+            wait_slots(c_in, sem, 31)
+
+    wait_cols(cr_sem)
+    wait_slots(r_in, rr_sem, 31)
     even = r_in[0]
     odd = r_in[1]
     for n in range(1, 16):
@@ -417,16 +468,12 @@
     tri = both[0:1, :V] + cols[0:1, :V] + at_hubs(1)
     deg = cols[1:2, :V] + at_hubs(2)
     out[...] = tri / (1.0 + deg)
-    for n in range(B // V):
-        for g in range(2):
-            @pl.when(jnp.logical_or(off, jnp.logical_or(n != c, g != h)))
-            def _(n=n, g=g):
-                to_owner(n, g).wait_send()
-
-    plane(lambda n: to_plane(n).wait_send())
-
-
-ROWS_TO, COLS_TO = destinations()
+    wait_cols(cs_sem)
+    wait_slots(r_in, rs_sem, 31)
+
+
+ROWS0_TO, ROWS1_TO, COLS_TO = destinations()
+MOST_SENDS = 1 + max(sum(bin(m).count("1") for m in masks) for masks in zip(ROWS0_TO, ROWS1_TO, COLS_TO))
 
 
 def body(light_bits, hub_bits, hub_ids):
@@ -463,16 +510,16 @@
             pltpu.VMEM((32, 4, 128), F32),
             pltpu.VMEM((32, 2, 128), F32),
             pltpu.SemaphoreType.DMA((4,)),
-            pltpu.SemaphoreType.DMA((33,)),
+            pltpu.SemaphoreType.DMA((MOST_SENDS,)),
             pltpu.SemaphoreType.DMA((6,)),
             pltpu.SemaphoreType.DMA((16,)),
             pltpu.SemaphoreType.DMA((2,)),
-            pltpu.SemaphoreType.DMA((8,)),
-            pltpu.SemaphoreType.DMA((8,)),
-            pltpu.SemaphoreType.DMA((32,)),
-            pltpu.SemaphoreType.DMA((32,)),
-            pltpu.SemaphoreType.DMA((32,)),
-            pltpu.SemaphoreType.DMA((32,)),
+            pltpu.SemaphoreType.DMA,
+            pltpu.SemaphoreType.DMA,
+            pltpu.SemaphoreType.DMA,
+            pltpu.SemaphoreType.DMA,
+            pltpu.SemaphoreType.DMA,
+            pltpu.SemaphoreType.DMA,
         ],
         compiler_params=pltpu.CompilerParams(
             collective_id=0, has_side_effects=True, vmem_limit_bytes=67043328

time: 39.4 us -> 36.6 us (0.929)
  the two profiles are of different devices: /device:TPU:24 before, /device:TPU:8 now
where the time goes in v3:
time: 36.6 us; the launch traced here: 36.4 us
  Pallas kernels  35.3 us (96%)
  local copies, waits for them, and re-layouts  1.1 us (3%)
    pallas_call x1, Pallas kernels, body(): pl.pallas_call(kernel, out_shape=jax.ShapeDtypeStruct((1, V), F32), in_sp...  35.3 us
    unnamed x3, local copies, waits for them, and re-layouts  1.1 us

profile of v3, /device:TPU:8, one launch (start us, length us, event | category | flops | bytes accessed | tf_op | source)
XLA Modules:
  0.0 36.4 jit_solution(4173046428554610062)
XLA Ops:
  0.0 35.3 %shard_map.37 = f32[1,96]{1,0:T(1,128)} custom-call(s32[48,768]{1,0:T(8,128)} %lb.1, s32[4,768]{1,0:T(4,128)} %hb.1, s32[2,128]{1,0:T(2,128)} %bitcast.2), custom_call_target="tpu_custom_call" | custom-call | tf_op jit(solution)/shard_map/pallas_call | solution.py:485
  35.3 0.0 copy-start
  35.3 0.6 %copy-done = f32[1,96]{1,0:T(1,128)S(1)} copy-done((f32[1,96]{1,0:T(1,128)S(1)}, f32[1,96]{1,0:T(1,128)}, u32[]{:S(2)}) %copy-start) | copy-done | bytes 408
  35.9 0.5 %copy.5 = f32[96]{0:T(128)} copy(f32[96]{0:T(128)S(1)} %bitcast.3) | data formatting | bytes 768
Async XLA Ops:
  35.3 0.6 %copy-start = (f32[1,96]{1,0:T(1,128)S(1)}, f32[1,96]{1,0:T(1,128)}, u32[]{:S(2)}) copy-start(f32[1,96]{1,0:T(1,128)} %shard_map.37) | copy-start | bytes 1156

commit v4 on v3

--- a/solution.py
+++ b/solution.py
@@ -12,14 +12,14 @@
 F8 = jnp.float8_e4m3fn
 
 THIRD = [
-    0, 0, 47, 3, 42, 35, 59, 41, 28, 46, 60, 43, 52, 59, 46, 23,
-    52, 17, 9, 9, 22, 4, 37, 26, 53, 34, 47, 20, 39, 22, 53, 59,
-    62, 1, 11, 47, 18, 18, 17, 61, 4, 61, 33, 47, 48, 15, 37, 55,
-    48, 20, 62, 1, 3, 38, 27, 27, 40, 52, 13, 52, 47, 52, 14, 56,
-    15, 2, 25, 7, 11, 22, 11, 23, 36, 36, 25, 60, 62, 1, 59, 41,
-    16, 49, 48, 11, 16, 51, 24, 58, 2, 46, 45, 45, 20, 48, 14, 7,
-    13, 2, 13, 24, 35, 21, 1, 19, 42, 35, 43, 57, 54, 54, 46, 11,
-    32, 25, 32, 17, 8, 26, 26, 44, 22, 4, 26, 44, 60, 16, 63, 63,
+    0, 0, 43, 57, 26, 55, 15, 43, 13, 35, 47, 11, 20, 62, 41, 31,
+    16, 52, 9, 9, 38, 16, 21, 28, 34, 6, 2, 46, 52, 2, 60, 53,
+    13, 32, 11, 47, 18, 18, 13, 31, 48, 39, 57, 29, 40, 55, 47, 25,
+    50, 4, 57, 6, 6, 20, 27, 27, 12, 2, 20, 46, 48, 20, 10, 60,
+    22, 7, 31, 13, 26, 13, 47, 51, 36, 36, 26, 47, 51, 40, 51, 57,
+    48, 34, 33, 59, 4, 50, 3, 15, 32, 49, 45, 45, 22, 4, 8, 31,
+    8, 29, 29, 57, 33, 26, 31, 41, 15, 34, 61, 11, 54, 54, 31, 41,
+    20, 48, 1, 19, 2, 52, 51, 5, 20, 5, 22, 44, 32, 50, 63, 63,
 ]
 
 
@@ -43,7 +43,7 @@
                     if i != j and k != j:
                         rows[h][(i * 8 + k) * 2 + nearer(j, k, h)] |= 1 << (2 * j + s)
                     if i != j and k != i:
-                        cols[(k * 8 + j) * 2 + h] |= 1 << (2 * i + s)
+                        cols[((k * 8 + j) * 2 + h)] |= 1 << (8 * s + i)
     return rows[0], rows[1], cols
 
 
@@ -83,8 +83,8 @@
 
 def kernel(
     lb, hb, ids, out,
-    ids_s, ids_v, m1, m2, m3, mm1, hubw, hub_i, a8, b8, o8, r8,
-    acc_r, acc_c, col, hpart, h_in, rmsg, cmsg, r_in, c_in,
+    ids_s, ids_v, m1, m2, m3, mm1, hubw, hub_i, a0, a1, a2, a3, a4, a5, b_own, b_other, o8, r8,
+    acc_r, col, hpart, h_in, rmsg, cmsg, r_in, c_in,
     local_sem, send_sem, recv_sem, hub_send, hub_recv, ha_send, ha_recv, rs_sem, rr_sem, cs_sem, cr_sem,
 ):
     I = lax.axis_index("rows")
@@ -99,6 +99,7 @@
     V = out.shape[1]
     diag = I == J
     off = jnp.logical_not(diag)
+    me = c * 2 + h
 
     loads = [
         pltpu.make_async_copy(lb, m1.at[s], local_sem.at[0]),
@@ -109,25 +110,45 @@
     for load in loads:
         load.start()
 
+    (thirds,) = lookup([THIRD], (I * 8 + J) * 2 + h, 7)
+    K = lax.rem(jnp.where(s == 1, lax.div(thirds, 8), thirds), 8)
+    ahead = lax.rem(lax.div(K, 2) - lax.div(J, 2) + 4, 4)
+    near = jnp.where(ahead == 0, h, jnp.where(ahead == 1, 0, jnp.where(ahead == 3, 1, 1 - h)))
+
     barrier = pltpu.get_barrier_semaphore()
 
     def signal(dev):
         pl.semaphore_signal(barrier, inc=1, device_id=dev, device_id_type=MESH)
 
-    me = c * 2 + h
-    for n in range(1, 32):
-        peer = lax.rem(me + n, 32)
-        signal((I, lax.div(peer, 2), lax.rem(peer, 2)))
+    signal((I, c + 1 - 2 * s, h))
+
+    @pl.when(jnp.logical_and(off, K != J))
+    def _():
+        for x in range(2):
+            signal((I, 2 * K + x, near))
+
+    @pl.when(jnp.logical_and(off, K != I))
+    def _():
+        signal((K, c, h))
+
     for n in range(1, 8):
-        for half in range(2):
-            signal((lax.rem(I + n, 8), 2 * J + half, h))
-
-    to_rows0, to_rows1, to_cols, thirds = lookup([ROWS0_TO, ROWS1_TO, COLS_TO, THIRD], (I * 8 + J) * 2 + h, 7)
-    K = lax.rem(jnp.where(s == 1, lax.div(thirds, 8), thirds), 8)
-    K_twin = lax.rem(jnp.where(s == 0, lax.div(thirds, 8), thirds), 8)
+        signal((lax.rem(I + n, 8), c, h))
+    for x in range(2):
+        for g in range(2):
+            @pl.when(jnp.logical_or(off, jnp.logical_or(s != x, h != g)))
+            def _(x=x, g=g):
+                signal((I, 2 * I + x, g))
+
+    to_rows0, to_rows1, to_cols = lookup([ROWS0_TO, ROWS1_TO, COLS_TO], (I * 8 + J) * 2 + h, 7)
+    to_cols = lax.rem(jnp.where(s == 1, lax.div(to_cols, 256), to_cols), 256)
+    readers = 0
+    for mask, count in ((to_rows0, 16), (to_rows1, 16), (to_cols, 8)):
+        for n in range(count):
+            readers = readers + lax.rem(lax.div(mask, 2**n), 2)
+    greeted = readers + jnp.where(diag, 39, 8)
     loads[0].wait()
     loads[1].wait()
-    pl.semaphore_wait(barrier, 45)
+    pl.semaphore_wait(barrier, greeted)
 
     own = m1.at[s]
 
@@ -136,13 +157,13 @@
             own, m2.at[s], send_sem.at[sem], recv_sem.at[2 + s], device_id=(I, n, g), device_id_type=MESH
         )
 
-    def to_col(n, sem):
-        return pltpu.make_async_remote_copy(
-            own,
-            m3.at[s],
+    def to_col(n, half, sem):
+        return pltpu.make_async_remote_copy(
+            m1.at[half],
+            m3.at[half],
             send_sem.at[sem],
-            recv_sem.at[4 + s],
-            device_id=(n // 2, 2 * J + n % 2, h),
+            recv_sem.at[4 + half],
+            device_id=(n, c, h),
             device_id_type=MESH,
         )
 
@@ -165,7 +186,17 @@
                     act(to_hub(n))
 
     each_hub(lambda d: d.start())
+    to_twin().start()
     sent = jnp.int32(1)
+    for n in range(8):
+        go = bit_of(to_cols, n)
+
+        @pl.when(go)
+        def _(n=n, sent=sent):
+            to_col(n, s, sent).start()
+
+        sent = sent + go.astype(jnp.int32)
+
     for g, mask in enumerate((to_rows0, to_rows1)):
         for n in range(16):
             go = bit_of(mask, n)
@@ -175,19 +206,6 @@
                 to_row(n, g, sent).start()
 
             sent = sent + go.astype(jnp.int32)
-
-    for n in range(16):
-        go = jnp.logical_and(bit_of(to_cols, n), s == n % 2)
-
-        @pl.when(go)
-        def _(n=n, sent=sent):
-            to_col(n, sent).start()
-
-        sent = sent + go.astype(jnp.int32)
-
-    @pl.when(K_twin == J)
-    def _():
-        to_twin().start()
 
     loads[2].wait()
     loads[3].wait()
@@ -213,6 +231,7 @@
     keep_words = jnp.bitwise_not(words)
     keep_i = jnp.broadcast_to(keep_words[0:1, :], (128, 128)).T[:W]
     keep_k = jnp.broadcast_to(keep_words[1:2, :], (128, 128)).T[:W]
+    keep_k_wide = jnp.concatenate([keep_k] * (C // 128), axis=1)
     keep_col = flags - 1
 
     def keep_cols_of(half, t):
@@ -227,94 +246,13 @@
     mask_half(s)
     unpack_into(o8, mm1.at[s], W)
 
-    @pl.when(diag)
-    def _():
-        hub_i[s] = hubw[...]
-
-    def hub_half(half):
-        pltpu.make_async_copy(hubw, hub_i.at[half], hub_recv.at[half]).wait()
-
-    @pl.when(off)
-    def _():
-        hub_half(s)
-
-    hub_half(o)
-    G = hubw.shape[0]
-    for half in range(2):
-        for n, bits in enumerate(rows_of_bits(hub_i[half], 0, G)):
-            r8[n * 32 : n * 32 + 32, half * C : half * C + C] = bits.astype(F32).astype(F8)
-    reach = jnp.dot(r8[...], o8[...], preferred_element_type=F32)
-    edge = hubw[...]
-    lanes_c = jnp.concatenate([keep_cols_of(s, t) for t in range(C // 128)], axis=1)
-    edge = edge & lanes_c
-    hub_bits = jnp.concatenate(rows_of_bits(edge, 0, G), axis=0)
-    meet = jnp.where(hub_bits != 0, reach, 0.0)
-    hub_flag = hub_bits.astype(F32)
-
-    def across(x):
-        t = x[:, 0:128]
-        for n in range(1, x.shape[1] // 128):
-            t = t + x[:, n * 128 : n * 128 + 128]
-        return jnp.sum(t.T, axis=0, keepdims=True)
-
-    hub_tri = 0.5 * across(meet)
-    hub_deg = across(hub_flag)
-    hpart[...] = hub_tri
-
-    def to_column(n):
-        return pltpu.make_async_remote_copy(
-            hpart, h_in.at[I], ha_send, ha_recv, device_id=(n, c, h), device_id_type=MESH
-        )
-
-    def others(act):
-        for n in range(8):
-            @pl.when(n != I)
-            def _(n=n):
-                act(n)
-
-    others(lambda n: to_column(n).start())
-
-    light_deg = jnp.sum(lax.population_count(mm1[s]).astype(F32), axis=0, keepdims=True) * 0.5
-    edge_deg = jnp.sum(lax.population_count(edge).astype(F32), axis=0, keepdims=True)
-    col[0:1, :] = jnp.sum(meet, axis=0, keepdims=True)
-    col[1:2, :] = light_deg + jnp.where(diag, 1.0, 0.0) * edge_deg
-
     def recv(ref, sem):
         pltpu.make_async_copy(own, ref, sem).wait()
 
-    for n in range(16):
-        go = jnp.logical_and(bit_of(to_cols, n), s != n % 2)
-
-        @pl.when(go)
-        def _(n=n, sent=sent):
-            to_col(n, sent).start()
-
-        sent = sent + go.astype(jnp.int32)
-
-    @pl.when(K_twin != J)
-    def _():
-        to_twin().start()
-
-    @pl.when(K != J)
-    def _():
-        recv(m2.at[0], recv_sem.at[2])
-
-    @pl.when(K == J)
-    def _():
-        recv(m1.at[o], recv_sem.at[o])
-        m2[...] = m1[...]
-
-    unpack_into(a8, m2.at[0], W, 0)
-    @pl.when(K != J)
-    def _():
-        recv(m2.at[1], recv_sem.at[3])
-
-    unpack_into(a8, m2.at[1], W, C)
-    acc_r[...] = jnp.zeros_like(acc_r)
+    rows_ik = (a0, a1, a2, a3, a4, a5)
     row_w = jnp.where(diag, 0.125, jnp.where(K == I, 1.0, 0.5))
     col_w = jnp.where(diag, 0.0, jnp.where(K == J, 1.0, 0.5))
     MC = 256
-    shift = lax.broadcasted_iota(jnp.int32, (32, C), 0)
 
     def to_owner(n, k):
         return pltpu.make_async_remote_copy(
@@ -326,7 +264,7 @@
             device_id_type=MESH,
         )
 
-    def face(half, name):
+    def kj(half, name):
         @pl.when(K != I)
         def _():
             recv(m3.at[half], recv_sem.at[4 + half])
@@ -335,37 +273,36 @@
         def _():
             m3[half] = m1[half]
 
-        for t in range(C // 128):
-            at = slice(t * 128, t * 128 + 128)
-            m3[half, :, at] = m3[half, :, at] & keep_k
-        unpack_into(b8.at[half], m3.at[half], W)
-
-        acc_c[...] = jnp.zeros_like(acc_c)
-
-        def chunk(g, carry):
-            sums = acc_c[...]
-            for u in range(2):
-                m = g * 2 + u
-                paths = jnp.dot(
-                    a8[pl.ds(pl.multiple_of(m * MC, MC), MC), :], b8[half], preferred_element_type=F32
-                )
-                words = mm1[half, pl.ds(pl.multiple_of(m * (MC // 32), MC // 32), MC // 32), :]
-                for w in range(MC // 32):
-                    x = jnp.broadcast_to(words[w : w + 1, :], (32, C))
-                    bits = jnp.bitwise_and(jnp.right_shift(x, shift), 1)
-                    t = jnp.where(bits != 0, paths[w * 32 : w * 32 + 32], 0.0)
-                    sums = sums + jnp.sum(t.reshape(4, 8, C), axis=0)
-                    row = t[:, 0:128]
-                    for q in range(1, C // 128):
-                        row = row + t[:, q * 128 : q * 128 + 128]
-                    acc_r[pl.ds(pl.multiple_of(m * MC + w * 32, 32), 32), :] += row
-            acc_c[...] = sums
-            return carry
-
-        lax.fori_loop(0, B // (2 * MC), chunk, 0)
-
-    def send_cols(half, first):
-        whole = col_w * jnp.sum(acc_c[...], axis=0, keepdims=True)
+
+    def kj_words(dst, half, first, count):
+        for g in range(first, first + count, 8):
+            words = m3[half, g : g + 8, :] & keep_k_wide[g : g + 8, :]
+            for n, bits in enumerate(rows_of_bits(words, 0, 8)):
+                dst[(g + n) * 32 : (g + n) * 32 + 32, :] = bits.astype(F32).astype(F8)
+
+    def ik_rows(m):
+        for half in range(2):
+            words = m2[half, m * 8 : m * 8 + 8, :]
+            for n, bits in enumerate(rows_of_bits(words, 0, 8)):
+                rows_ik[m][n * 32 : n * 32 + 32, half * C : half * C + C] = bits.astype(F32).astype(F8)
+
+    def product(m, b8, half, first, beside):
+        paths = jnp.dot(rows_ik[m][...], b8[...], preferred_element_type=F32)
+        beside()
+        words = mm1[half, m * 8 : m * 8 + 8, :]
+        sums = jnp.zeros((8, C), F32)
+        for w, bits in enumerate(rows_of_bits(words, 0, 8)):
+            t = jnp.where(bits != 0, paths[w * 32 : w * 32 + 32], 0.0)
+            sums = sums + jnp.sum(t.reshape(4, 8, C), axis=0)
+            row = t[:, 0:128]
+            for q in range(1, C // 128):
+                row = row + t[:, q * 128 : q * 128 + 128]
+            at = slice(m * MC + w * 32, m * MC + w * 32 + 32)
+            acc_r[at, :] = row if first else acc_r[at, :] + row
+        return sums
+
+    def send_cols(half, sums, first):
+        whole = col_w * sums
         if first:
             whole = whole + col[0:1, :]
         for k in range(C // V):
@@ -382,17 +319,104 @@
                 def _(n=n, g=g):
                     to_owner(n, g).start()
 
-    face(s, "p13")
+    kj(s, "p10")
+    kj_words(b_own, s, 0, W)
+    recv(m1.at[o], recv_sem.at[o])
+    for n in range(8):
+        go = bit_of(to_cols, n)
+
+        @pl.when(go)
+        def _(n=n, sent=sent):
+            to_col(n, o, sent).start()
+
+        sent = sent + go.astype(jnp.int32)
+
+    @pl.when(diag)
+    def _():
+        hub_i[s] = hubw[...]
+
+    def hub_half(half):
+        pltpu.make_async_copy(hubw, hub_i.at[half], hub_recv.at[half]).wait()
+
+    @pl.when(off)
+    def _():
+        hub_half(s)
+
+    hub_half(o)
+    G = hubw.shape[0]
+    for half in range(2):
+        for n, bits in enumerate(rows_of_bits(hub_i[half], 0, G)):
+            r8[n * 32 : n * 32 + 32, half * C : half * C + C] = bits.astype(F32).astype(F8)
+    reach = jnp.dot(r8[...], o8[...], preferred_element_type=F32)
+    edge = hubw[...]
+    lanes_c = jnp.concatenate([keep_cols_of(s, t) for t in range(C // 128)], axis=1)
+    edge = edge & lanes_c
+    hub_bits = jnp.concatenate(rows_of_bits(edge, 0, G), axis=0)
+    meet = jnp.where(hub_bits != 0, reach, 0.0)
+    hub_flag = hub_bits.astype(F32)
+
+    def across(x):
+        t = x[:, 0:128]
+        for n in range(1, x.shape[1] // 128):
+            t = t + x[:, n * 128 : n * 128 + 128]
+        return jnp.sum(t.T, axis=0, keepdims=True)
+
+    hub_tri = 0.5 * across(meet)
+    hub_deg = across(hub_flag)
+    hpart[...] = hub_tri
+
+    def to_column(n):
+        return pltpu.make_async_remote_copy(
+            hpart, h_in.at[I], ha_send, ha_recv, device_id=(n, c, h), device_id_type=MESH
+        )
+
+    def others(act):
+        for n in range(8):
+            @pl.when(n != I)
+            def _(n=n):
+                act(n)
+
+    others(lambda n: to_column(n).start())
+
+    light_deg = jnp.sum(lax.population_count(mm1[s]).astype(F32), axis=0, keepdims=True) * 0.5
+    edge_deg = jnp.sum(lax.population_count(edge).astype(F32), axis=0, keepdims=True)
+    col[0:1, :] = jnp.sum(meet, axis=0, keepdims=True)
+    col[1:2, :] = light_deg + jnp.where(diag, 1.0, 0.0) * edge_deg
+
+    @pl.when(K != J)
+    def _():
+        recv(m2.at[0], recv_sem.at[2])
+
+    @pl.when(K == J)
+    def _():
+        m2[...] = m1[...]
+
+    @pl.when(K != J)
+    def _():
+        recv(m2.at[1], recv_sem.at[3])
+
+    ik_rows(0)
+    col_own = jnp.zeros((8, C), F32)
+    for m in range(6):
+        if m == 3:
+            mask_half(o)
+            kj(o, "p14")
+
+        def beside(m=m):
+            if m < 5:
+                ik_rows(m + 1)
+            if m >= 3:
+                kj_words(b_other, o, (m - 3) * 16, 16)
+
+        col_own = col_own + product(m, b_own, s, True, beside)
+    sums = jnp.sum(col_own, axis=0, keepdims=True)
+    col_other = jnp.zeros((8, C), F32)
+    for m in range(6):
+        col_other = col_other + product(m, b_other, o, False, lambda: None)
     pltpu.make_async_copy(h_in.at[pl.ds(0, 7)], h_in.at[pl.ds(0, 7)], ha_recv).wait()
     h_in[I] = hpart[...]
-    send_cols(s, True)
-    @pl.when(K != J)
-    def _():
-        recv(m1.at[o], recv_sem.at[o])
-
-    mask_half(o)
-    face(o, "p16")
-    send_cols(o, False)
+    send_cols(s, sums, True)
+    send_cols(o, jnp.sum(col_other, axis=0, keepdims=True), False)
 
     hub_all = h_in[0]
     for n in range(1, 8):
@@ -473,7 +497,11 @@
 
 
 ROWS0_TO, ROWS1_TO, COLS_TO = destinations()
-MOST_SENDS = 1 + max(sum(bin(m).count("1") for m in masks) for masks in zip(ROWS0_TO, ROWS1_TO, COLS_TO))
+MOST_SENDS = 1 + max(
+    sum(bin(x).count("1") for x in (r0, r1, *[c >> (8 * s) & 255 for s in (half, half)]))
+    for r0, r1, c in zip(ROWS0_TO, ROWS1_TO, COLS_TO)
+    for half in range(2)
+)
 
 
 def body(light_bits, hub_bits, hub_ids):
@@ -496,12 +524,12 @@
             pltpu.VMEM((2, W, C), jnp.int32),
             pltpu.VMEM((G, C), jnp.int32),
             pltpu.VMEM((2, G, C), jnp.int32),
-            pltpu.VMEM((B, B), F8),
-            pltpu.VMEM((2, B, C), F8),
+            *[pltpu.VMEM((B // 6, B), F8)] * 6,
+            pltpu.VMEM((B, C), F8),
+            pltpu.VMEM((B, C), F8),
             pltpu.VMEM((B, C), F8),
             pltpu.VMEM((32 * G, B), F8),
             pltpu.VMEM((B, 128), F32),
-            pltpu.VMEM((8, C), F32),
             pltpu.VMEM((2, C), F32),
             pltpu.VMEM((1, 128), F32),
             pltpu.VMEM((8, 1, 128), F32),

time: 36.6 us -> 33.6 us (0.918)
  the two profiles are of different devices: /device:TPU:8 before, /device:TPU:9 now
where the time goes in v4:
time: 33.6 us; the launch traced here: 33.5 us
  Pallas kernels  32.3 us (96%)
  local copies, waits for them, and re-layouts  1.1 us (3%)
    pallas_call x1, Pallas kernels, body(): pl.pallas_call(kernel, out_shape=jax.ShapeDtypeStruct((1, V), F32), in_sp...  32.3 us
    unnamed x3, local copies, waits for them, and re-layouts  1.1 us

profile of v4, /device:TPU:9, one launch (start us, length us, event | category | flops | bytes accessed | tf_op | source)
XLA Modules:
  0.0 33.5 jit_solution(8836577257429654525)
XLA Ops:
  0.0 32.3 %shard_map.37 = f32[1,96]{1,0:T(1,128)} custom-call(s32[48,768]{1,0:T(8,128)} %lb.1, s32[4,768]{1,0:T(4,128)} %hb.1, s32[2,128]{1,0:T(2,128)} %bitcast.2), custom_call_target="tpu_custom_call" | custom-call | tf_op jit(solution)/shard_map/pallas_call | solution.py:513
  32.3 0.0 copy-start
  32.4 0.6 %copy-done = f32[1,96]{1,0:T(1,128)S(1)} copy-done((f32[1,96]{1,0:T(1,128)S(1)}, f32[1,96]{1,0:T(1,128)}, u32[]{:S(2)}) %copy-start) | copy-done | bytes 408
  32.9 0.5 %copy.5 = f32[96]{0:T(128)} copy(f32[96]{0:T(128)S(1)} %bitcast.3) | data formatting | bytes 768
Async XLA Ops:
  32.3 0.6 %copy-start = (f32[1,96]{1,0:T(1,128)S(1)}, f32[1,96]{1,0:T(1,128)}, u32[]{:S(2)}) copy-start(f32[1,96]{1,0:T(1,128)} %shard_map.37) | copy-start | bytes 1156

commit v5 on v4

--- a/solution.py
+++ b/solution.py
@@ -12,14 +12,14 @@
 F8 = jnp.float8_e4m3fn
 
 THIRD = [
-    0, 0, 43, 57, 26, 55, 15, 43, 13, 35, 47, 11, 20, 62, 41, 31,
-    16, 52, 9, 9, 38, 16, 21, 28, 34, 6, 2, 46, 52, 2, 60, 53,
-    13, 32, 11, 47, 18, 18, 13, 31, 48, 39, 57, 29, 40, 55, 47, 25,
-    50, 4, 57, 6, 6, 20, 27, 27, 12, 2, 20, 46, 48, 20, 10, 60,
-    22, 7, 31, 13, 26, 13, 47, 51, 36, 36, 26, 47, 51, 40, 51, 57,
-    48, 34, 33, 59, 4, 50, 3, 15, 32, 49, 45, 45, 22, 4, 8, 31,
-    8, 29, 29, 57, 33, 26, 31, 41, 15, 34, 61, 11, 54, 54, 31, 41,
-    20, 48, 1, 19, 2, 52, 51, 5, 20, 5, 22, 44, 32, 50, 63, 63,
+    0, 0, 47, 3, 42, 35, 59, 41, 28, 46, 60, 43, 52, 59, 46, 23,
+    52, 17, 9, 9, 22, 4, 37, 26, 53, 34, 47, 20, 39, 22, 53, 59,
+    62, 1, 11, 47, 18, 18, 17, 61, 4, 61, 33, 47, 48, 15, 37, 55,
+    48, 20, 62, 1, 3, 38, 27, 27, 40, 52, 13, 52, 47, 52, 14, 56,
+    15, 2, 25, 7, 11, 22, 11, 23, 36, 36, 25, 60, 62, 1, 59, 41,
+    16, 49, 48, 11, 16, 51, 24, 58, 2, 46, 45, 45, 20, 48, 14, 7,
+    13, 2, 13, 24, 35, 21, 1, 19, 42, 35, 43, 57, 54, 54, 46, 11,
+    32, 25, 32, 17, 8, 26, 26, 44, 22, 4, 26, 44, 60, 16, 63, 63,
 ]
 
 
@@ -85,7 +85,7 @@
     lb, hb, ids, out,
     ids_s, ids_v, m1, m2, m3, mm1, hubw, hub_i, a0, a1, a2, a3, a4, a5, b_own, b_other, o8, r8,
     acc_r, col, hpart, h_in, rmsg, cmsg, r_in, c_in,
-    local_sem, send_sem, recv_sem, hub_send, hub_recv, ha_send, ha_recv, rs_sem, rr_sem, cs_sem, cr_sem,
+    local_sem, send_sem, recv_sem, twin_sem, hub_send, hub_recv, ha_send, ha_recv, rs_sem, rr_sem, cs_sem, cr_sem,
 ):
     I = lax.axis_index("rows")
     c = lax.axis_index("cols")
@@ -110,18 +110,20 @@
     for load in loads:
         load.start()
 
+    barrier = pltpu.get_barrier_semaphore()
+
+    def signal(dev):
+        pl.semaphore_signal(barrier, inc=1, device_id=dev, device_id_type=MESH)
+
+    signal((I, c + 1 - 2 * s, h))
+
+    for n in range(1, 8):
+        signal((lax.rem(I + n, 8), c, h))
     (thirds,) = lookup([THIRD], (I * 8 + J) * 2 + h, 7)
     K = lax.rem(jnp.where(s == 1, lax.div(thirds, 8), thirds), 8)
     ahead = lax.rem(lax.div(K, 2) - lax.div(J, 2) + 4, 4)
     near = jnp.where(ahead == 0, h, jnp.where(ahead == 1, 0, jnp.where(ahead == 3, 1, 1 - h)))
 
-    barrier = pltpu.get_barrier_semaphore()
-
-    def signal(dev):
-        pl.semaphore_signal(barrier, inc=1, device_id=dev, device_id_type=MESH)
-
-    signal((I, c + 1 - 2 * s, h))
-
     @pl.when(jnp.logical_and(off, K != J))
     def _():
         for x in range(2):
@@ -131,8 +133,6 @@
     def _():
         signal((K, c, h))
 
-    for n in range(1, 8):
-        signal((lax.rem(I + n, 8), c, h))
     for x in range(2):
         for g in range(2):
             @pl.when(jnp.logical_or(off, jnp.logical_or(s != x, h != g)))
@@ -157,19 +157,26 @@
             own, m2.at[s], send_sem.at[sem], recv_sem.at[2 + s], device_id=(I, n, g), device_id_type=MESH
         )
 
-    def to_col(n, half, sem):
-        return pltpu.make_async_remote_copy(
-            m1.at[half],
-            m3.at[half],
+    def to_col(n, half, sem, rows=None):
+        return pltpu.make_async_remote_copy(
+            m1.at[half] if rows is None else m1.at[half, rows],
+            m3.at[half] if rows is None else m3.at[half, rows],
             send_sem.at[sem],
             recv_sem.at[4 + half],
             device_id=(n, c, h),
             device_id_type=MESH,
         )
 
-    def to_twin():
-        return pltpu.make_async_remote_copy(
-            own, m1.at[s], send_sem.at[0], recv_sem.at[s], device_id=(I, c + 1 - 2 * s, h), device_id_type=MESH
+    pieces = [pl.ds(p * (W // 2), W // 2) for p in range(2)]
+
+    def to_twin(p):
+        return pltpu.make_async_remote_copy(
+            m1.at[s, pieces[p]],
+            m1.at[s, pieces[p]],
+            send_sem.at[0],
+            twin_sem.at[p],
+            device_id=(I, c + 1 - 2 * s, h),
+            device_id_type=MESH,
         )
 
     def to_hub(n):
@@ -186,7 +193,8 @@
                     act(to_hub(n))
 
     each_hub(lambda d: d.start())
-    to_twin().start()
+    to_twin(0).start()
+    to_twin(1).start()
     sent = jnp.int32(1)
     for n in range(8):
         go = bit_of(to_cols, n)
@@ -319,18 +327,22 @@
                 def _(n=n, g=g):
                     to_owner(n, g).start()
 
+    sent0 = sent
+    for p in range(2):
+        part = m1.at[o, pieces[p]]
+        pltpu.make_async_copy(part, part, twin_sem.at[p]).wait()
+        sent = sent0
+        for n in range(8):
+            go = bit_of(to_cols, n)
+
+            @pl.when(go)
+            def _(n=n, sent=sent, p=p):
+                to_col(n, o, sent, pieces[p]).start()
+
+            sent = sent + go.astype(jnp.int32)
+
     kj(s, "p10")
     kj_words(b_own, s, 0, W)
-    recv(m1.at[o], recv_sem.at[o])
-    for n in range(8):
-        go = bit_of(to_cols, n)
-
-        @pl.when(go)
-        def _(n=n, sent=sent):
-            to_col(n, o, sent).start()
-
-        sent = sent + go.astype(jnp.int32)
-
     @pl.when(diag)
     def _():
         hub_i[s] = hubw[...]
@@ -411,18 +423,24 @@
         col_own = col_own + product(m, b_own, s, True, beside)
     sums = jnp.sum(col_own, axis=0, keepdims=True)
     col_other = jnp.zeros((8, C), F32)
+
+    def row_sums(first, last):
+        for n in range(B // V):
+            if first * MC < n * V + V <= last * MC:
+                rmsg[n, 0:1, 0:V] = jnp.sum(acc_r[n * V : n * V + V, :].T, axis=0, keepdims=True) * row_w
+
     for m in range(6):
-        col_other = col_other + product(m, b_other, o, False, lambda: None)
+        col_other = col_other + product(m, b_other, o, False, lambda m=m: row_sums(m - 1, m))
     pltpu.make_async_copy(h_in.at[pl.ds(0, 7)], h_in.at[pl.ds(0, 7)], ha_recv).wait()
     h_in[I] = hpart[...]
     send_cols(s, sums, True)
     send_cols(o, jnp.sum(col_other, axis=0, keepdims=True), False)
 
+    row_sums(5, 6)
     hub_all = h_in[0]
     for n in range(1, 8):
         hub_all = hub_all + h_in[n]
     for n in range(B // V):
-        rmsg[n, 0:1, 0:V] = jnp.sum(acc_r[n * V : n * V + V, :].T, axis=0, keepdims=True) * row_w
         rmsg[n, 1:2, :] = hub_all
         rmsg[n, 2:3, :] = hub_deg
 
@@ -540,6 +558,7 @@
             pltpu.SemaphoreType.DMA((4,)),
             pltpu.SemaphoreType.DMA((MOST_SENDS,)),
             pltpu.SemaphoreType.DMA((6,)),
+            pltpu.SemaphoreType.DMA((2,)),
             pltpu.SemaphoreType.DMA((16,)),
             pltpu.SemaphoreType.DMA((2,)),
             pltpu.SemaphoreType.DMA,
@@ -550,7 +569,7 @@
             pltpu.SemaphoreType.DMA,
         ],
         compiler_params=pltpu.CompilerParams(
-            collective_id=0, has_side_effects=True, vmem_limit_bytes=67043328
+            collective_id=0, has_side_effects=True, vmem_limit_bytes=56550000
         ),
     )(light_bits, hub_bits, hub_ids.reshape(2, 128))
     return out.reshape(V)

time: 33.6 us -> 31.2 us (0.929)
  the two profiles are of different devices: /device:TPU:9 before, /device:TPU:8 now
where the time goes in v5:
time: 31.2 us; the launch traced here: 31.1 us
  Pallas kernels  30.6 us (98%)
  local copies, waits for them, and re-layouts  0.51 us (2%)
    pallas_call x1, Pallas kernels, body(): pl.pallas_call(kernel, out_shape=jax.ShapeDtypeStruct((1, V), F32), in_sp...  30.6 us

profile of v5, /device:TPU:8, one launch (start us, length us, event | category | flops | bytes accessed | tf_op | source)
XLA Modules:
  0.0 31.1 jit_solution(13238558746544307131)
XLA Ops:
  0.0 30.6 %shard_map.37 = f32[1,96]{1,0:T(1,128)S(1)} custom-call(s32[48,768]{1,0:T(8,128)} %lb.1, s32[4,768]{1,0:T(4,128)} %hb.1, s32[2,128]{1,0:T(2,128)} %bitcast.3), custom_call_target="tpu_custom_call" | custom-call | tf_op jit(solution)/shard_map/pallas_call | solution.py:531
  30.6 0.5 %copy.5 = f32[96]{0:T(128)} copy(f32[96]{0:T(128)S(1)} %bitcast.2) | data formatting | bytes 768

commit v6 on v5

--- a/solution.py
+++ b/solution.py
@@ -12,14 +12,14 @@
 F8 = jnp.float8_e4m3fn
 
 THIRD = [
-    0, 0, 47, 3, 42, 35, 59, 41, 28, 46, 60, 43, 52, 59, 46, 23,
-    52, 17, 9, 9, 22, 4, 37, 26, 53, 34, 47, 20, 39, 22, 53, 59,
-    62, 1, 11, 47, 18, 18, 17, 61, 4, 61, 33, 47, 48, 15, 37, 55,
-    48, 20, 62, 1, 3, 38, 27, 27, 40, 52, 13, 52, 47, 52, 14, 56,
-    15, 2, 25, 7, 11, 22, 11, 23, 36, 36, 25, 60, 62, 1, 59, 41,
-    16, 49, 48, 11, 16, 51, 24, 58, 2, 46, 45, 45, 20, 48, 14, 7,
-    13, 2, 13, 24, 35, 21, 1, 19, 42, 35, 43, 57, 54, 54, 46, 11,
-    32, 25, 32, 17, 8, 26, 26, 44, 22, 4, 26, 44, 60, 16, 63, 63,
+    0, 0, 57, 29, 42, 35, 47, 25, 55, 44, 11, 61, 44, 62, 15, 43,
+    48, 20, 9, 9, 6, 20, 19, 44, 32, 22, 46, 23, 6, 34, 37, 55,
+    14, 56, 57, 29, 18, 18, 25, 47, 37, 55, 41, 59, 53, 60, 57, 29,
+    48, 34, 7, 49, 16, 52, 27, 27, 6, 34, 12, 46, 32, 22, 44, 55,
+    17, 24, 43, 15, 24, 10, 13, 59, 36, 36, 25, 47, 30, 7, 43, 57,
+    4, 50, 24, 33, 2, 38, 19, 7, 16, 52, 45, 45, 50, 32, 7, 14,
+    1, 19, 29, 57, 17, 24, 41, 59, 10, 37, 29, 15, 54, 54, 29, 57,
+    34, 6, 8, 19, 4, 50, 10, 24, 20, 6, 35, 42, 34, 48, 63, 63,
 ]
 
 
@@ -85,7 +85,7 @@
     lb, hb, ids, out,
     ids_s, ids_v, m1, m2, m3, mm1, hubw, hub_i, a0, a1, a2, a3, a4, a5, b_own, b_other, o8, r8,
     acc_r, col, hpart, h_in, rmsg, cmsg, r_in, c_in,
-    local_sem, send_sem, recv_sem, twin_sem, hub_send, hub_recv, ha_send, ha_recv, rs_sem, rr_sem, cs_sem, cr_sem,
+    local_sem, send_sem, recv_sem, twin_sem, row_sem, hub_send, hub_recv, ha_send, ha_recv, rs_sem, rr_sem, cs_sem, cr_sem,
 ):
     I = lax.axis_index("rows")
     c = lax.axis_index("cols")
@@ -152,9 +152,16 @@
 
     own = m1.at[s]
 
-    def to_row(n, g, sem):
+    ik_pieces = [pl.ds(0, 2 * W // 3), pl.ds(2 * W // 3, W // 3)]
+
+    def to_row(n, g, sem, p):
         return pltpu.make_async_remote_copy(
-            own, m2.at[s], send_sem.at[sem], recv_sem.at[2 + s], device_id=(I, n, g), device_id_type=MESH
+            m1.at[s, ik_pieces[p]],
+            m2.at[s, ik_pieces[p]],
+            send_sem.at[sem],
+            row_sem.at[2 * p + s],
+            device_id=(I, n, g),
+            device_id_type=MESH,
         )
 
     def to_col(n, half, sem, rows=None):
@@ -205,15 +212,20 @@
 
         sent = sent + go.astype(jnp.int32)
 
-    for g, mask in enumerate((to_rows0, to_rows1)):
-        for n in range(16):
-            go = bit_of(mask, n)
-
-            @pl.when(go)
-            def _(n=n, g=g, sent=sent):
-                to_row(n, g, sent).start()
-
-            sent = sent + go.astype(jnp.int32)
+    def send_rows(p, sent):
+        for g, mask in enumerate((to_rows0, to_rows1)):
+            for n in range(16):
+                go = bit_of(mask, n)
+
+                @pl.when(go)
+                def _(n=n, g=g, sent=sent):
+                    to_row(n, g, sent, p).start()
+
+                sent = sent + go.astype(jnp.int32)
+        return sent
+
+    first_row = sent
+    sent = send_rows(0, first_row)
 
     loads[2].wait()
     loads[3].wait()
@@ -327,22 +339,27 @@
                 def _(n=n, g=g):
                     to_owner(n, g).start()
 
-    sent0 = sent
-    for p in range(2):
+    first_relay = sent
+
+    def relay(p):
         part = m1.at[o, pieces[p]]
         pltpu.make_async_copy(part, part, twin_sem.at[p]).wait()
-        sent = sent0
+        sent = first_relay
         for n in range(8):
             go = bit_of(to_cols, n)
 
             @pl.when(go)
-            def _(n=n, sent=sent, p=p):
+            def _(n=n, sent=sent):
                 to_col(n, o, sent, pieces[p]).start()
 
             sent = sent + go.astype(jnp.int32)
-
+        return sent
+
+    relay(0)
+    send_rows(1, first_row)
     kj(s, "p10")
     kj_words(b_own, s, 0, W)
+    sent = relay(1)
     @pl.when(diag)
     def _():
         hub_i[s] = hubw[...]
@@ -395,22 +412,28 @@
     col[0:1, :] = jnp.sum(meet, axis=0, keepdims=True)
     col[1:2, :] = light_deg + jnp.where(diag, 1.0, 0.0) * edge_deg
 
+
+    def ik_wait(p):
+        for half in range(2):
+            part = m2.at[half, ik_pieces[p]]
+            pltpu.make_async_copy(part, part, row_sem.at[2 * p + half]).wait()
+
     @pl.when(K != J)
     def _():
-        recv(m2.at[0], recv_sem.at[2])
+        ik_wait(0)
 
     @pl.when(K == J)
     def _():
         m2[...] = m1[...]
-
-    @pl.when(K != J)
-    def _():
-        recv(m2.at[1], recv_sem.at[3])
 
     ik_rows(0)
     col_own = jnp.zeros((8, C), F32)
     for m in range(6):
         if m == 3:
+            @pl.when(K != J)
+            def _():
+                ik_wait(1)
+
             mask_half(o)
             kj(o, "p14")
 
@@ -559,6 +582,7 @@
             pltpu.SemaphoreType.DMA((MOST_SENDS,)),
             pltpu.SemaphoreType.DMA((6,)),
             pltpu.SemaphoreType.DMA((2,)),
+            pltpu.SemaphoreType.DMA((4,)),
             pltpu.SemaphoreType.DMA((16,)),
             pltpu.SemaphoreType.DMA((2,)),
             pltpu.SemaphoreType.DMA,

time: 31.2 us -> 30.9 us (level)
  the two profiles are of different devices: /device:TPU:8 before, /device:TPU:17 now
where the time goes in v6:
time: 30.9 us; the launch traced here: 30.8 us
  Pallas kernels  30.2 us (98%)
  local copies, waits for them, and re-layouts  0.51 us (2%)
    pallas_call x1, Pallas kernels, body(): pl.pallas_call(kernel, out_shape=jax.ShapeDtypeStruct((1, V), F32), in_sp...  30.2 us

profile of v6, /device:TPU:17, one launch (start us, length us, event | category | flops | bytes accessed | tf_op | source)
XLA Modules:
  0.0 30.8 jit_solution(18002426886470088620)
XLA Ops:
  0.0 30.2 %shard_map.37 = f32[1,96]{1,0:T(1,128)S(1)} custom-call(s32[48,768]{1,0:T(8,128)} %lb.1, s32[4,768]{1,0:T(4,128)} %hb.1, s32[2,128]{1,0:T(2,128)} %bitcast.3), custom_call_target="tpu_custom_call" | custom-call | tf_op jit(solution)/shard_map/pallas_call | solution.py:554
  30.3 0.5 %copy.5 = f32[96]{0:T(128)} copy(f32[96]{0:T(128)S(1)} %bitcast.2) | data formatting | bytes 768
